TPU v7x, 128 devices: a whole 4x4x4 slice. The times are simulated.
128 devices in a mesh: coil: 32 (over x, y, z_lo), kz: 4 (over z_hi, core).
Axes of the slice: x: 4, y: 4, z: 4 (z_hi: 2, z_lo: 2; z = z_hi * 2 + z_lo), core: 2. Of those that a mesh axis runs over, the one named last changes fastest.
Arguments:
- kdata: bfloat16 [2, 64, 32, 256, 512], P(None, 'kz', 'coil'), may hold values from -6 to 6
- spoke_angle: int32 [256], replicated, may hold values from 0 to 63
- spoke_count: int32 [64], P('kz'), may hold values from 128 to 256
- block_index: int32 [64, 4], replicated, may hold values from 0 to 511
- interp: bfloat16 [64, 4, 128, 128], replicated, may hold values from -0.5 to 0.5
- sens_maps: bfloat16 [2, 32, 256, 256], P(None, 'coil'), may hold values from -2.5 to 2.5
Outputs:
- image: float32 [2, 64, 256, 256], P(None, 'kz', 'coil')
Inputs may be any that keep to these rules, and one draw needn't show every extreme that they name: Partition p uses its first spoke_count[p] spokes. `block_index`: several segments may hit the same grid block.
All inputs are finite; a program needn't handle non-finite values.
Results may differ from a plain program's by a relative error of at most 0.0059.
Values sent between devices are 32-bit elements; how exact they have to be, the bound alone decides.
A program may use at most 128 MiB of HBM per device.

v0:
```python
import jax
import jax.numpy as jnp
from jax import lax
from jax.sharding import PartitionSpec as P


def split_up(shard, dim, length):
    shape = shard.shape
    tiles = shard.reshape(*shape[:dim], length, shape[dim] // length, *shape[dim + 1 :])
    return jnp.moveaxis(tiles, dim, 0)


def sum_at_owner(shard, axis, dim):
    tiles = split_up(shard, dim, lax.axis_size(axis))
    arrived = lax.all_to_all(tiles, axis, split_axis=0, concat_axis=0, tiled=True)
    return arrived.sum(axis=0)


def in_order(tiles, dim):
    shape = list(tiles.shape[1:])
    shape[dim] *= tiles.shape[0]
    return jnp.moveaxis(tiles, 0, dim).reshape(shape)


def from_everyone(shard, axis):
    copies = jnp.broadcast_to(shard, (lax.axis_size(axis), *shard.shape))
    return lax.all_to_all(copies, axis, split_axis=0, concat_axis=0, tiled=True)


def collect(shard, axis, dim):
    return in_order(from_everyone(shard, axis), dim)


def dft_tables(length, dtype):
    index = jnp.arange(length, dtype=jnp.int32)
    product = index[:, None] * index[None, :] % length
    phase = product.astype(jnp.float32) * (2.0 * jnp.pi / length)
    scale = 1.0 / jnp.sqrt(jnp.float32(length))
    return ((jnp.cos(phase) * scale).astype(dtype), (jnp.sin(phase) * scale).astype(dtype))


def kz_block(z_first, z_count, k_count, length):
    z_index = z_first + jnp.arange(z_count, dtype=jnp.int32)
    k_index = jnp.arange(k_count, dtype=jnp.int32)
    product = z_index[:, None] * k_index[None, :] % length
    phase = product.astype(jnp.float32) * (2.0 * jnp.pi / length)
    scale = 1.0 / jnp.sqrt(jnp.float32(length))
    return (jnp.cos(phase) * scale, jnp.sin(phase) * scale)


def kz_apply(cos_z, sin_z, slab):
    high = lax.Precision.HIGHEST
    real_part = jnp.einsum("zk,kyx->zyx", cos_z, slab[0], precision=high) + jnp.einsum(
        "zk,kyx->zyx", sin_z, slab[1], precision=high
    )
    imag_part = jnp.einsum("zk,kyx->zyx", cos_z, slab[1], precision=high) - jnp.einsum(
        "zk,kyx->zyx", sin_z, slab[0], precision=high
    )
    return jnp.stack([real_part, imag_part])


def coil_image(data, weights, interp, block_index, cos_t, sin_t):
    f32 = jnp.float32
    binned = jnp.einsum("rpsn,psa->rpan", data, weights, preferred_element_type=f32).astype(
        jnp.bfloat16
    )
    rdim, pdim, adim, mdim = binned.shape
    seg = interp.shape[2]
    gdim = mdim // seg
    side = cos_t.shape[0]
    pieces = binned.reshape(rdim, pdim, adim, gdim, seg)
    contrib = jnp.einsum("rpagj,agjt->rpagt", pieces, interp, preferred_element_type=f32)
    flat = jnp.zeros((rdim, pdim, side * side // seg, seg), f32)
    flat = flat.at[:, :, block_index.reshape(-1)].add(contrib.reshape(rdim, pdim, adim * gdim, seg))
    grid = flat.reshape(rdim, pdim, side, side).astype(jnp.bfloat16)
    half_re = jnp.einsum("ky,pyx->pkx", cos_t, grid[0], preferred_element_type=f32) + jnp.einsum(
        "ky,pyx->pkx", sin_t, grid[1], preferred_element_type=f32
    )
    half_im = jnp.einsum("ky,pyx->pkx", cos_t, grid[1], preferred_element_type=f32) - jnp.einsum(
        "ky,pyx->pkx", sin_t, grid[0], preferred_element_type=f32
    )
    half_re = half_re.astype(jnp.bfloat16)
    half_im = half_im.astype(jnp.bfloat16)
    out_re = jnp.einsum("pkx,mx->pkm", half_re, cos_t, preferred_element_type=f32) + jnp.einsum(
        "pkx,mx->pkm", half_im, sin_t, preferred_element_type=f32
    )
    out_im = jnp.einsum("pkx,mx->pkm", half_im, cos_t, preferred_element_type=f32) - jnp.einsum(
        "pkx,mx->pkm", half_re, sin_t, preferred_element_type=f32
    )
    return jnp.stack([out_re, out_im])


def conj_product(sens, image):
    real_part = sens[0] * image[0] + sens[1] * image[1]
    imag_part = sens[0] * image[1] - sens[1] * image[0]
    return jnp.stack([real_part, imag_part])


def per_device(kdata, spoke_angle, spoke_count, block_index, interp, sens_maps):
    side = sens_maps.shape[2]
    parts_here = kdata.shape[1]
    spokes = kdata.shape[3]
    angles = interp.shape[0]
    cos_t, sin_t = dft_tables(side, jnp.bfloat16)
    position = jnp.arange(spokes, dtype=jnp.int32)
    used = position[None, :] < spoke_count[:, None]
    match = spoke_angle[:, None] == jnp.arange(angles, dtype=jnp.int32)[None, :]
    weights = (used[:, :, None] & match[None, :, :]).astype(jnp.bfloat16)
    data = kdata[:, :, 0]
    image_c = coil_image(data, weights, interp, block_index, cos_t, sin_t)
    sens_here = sens_maps.astype(jnp.float32)
    weighted = conj_product(sens_here[:, 0][:, None], image_c)
    combined = sum_at_owner(weighted, "coil", 2)
    groups = lax.axis_size("kz")
    kz_total = parts_here * groups
    my_first = lax.axis_index("kz") * parts_here
    piece = collect(combined, "kz", 1)
    cos_z, sin_z = kz_block(my_first, parts_here, piece.shape[1], kz_total)
    return kz_apply(cos_z, sin_z, piece)


def solution(mesh):
    placed = (
        P(None, "kz", "coil", None, None),
        P(),
        P("kz"),
        P(),
        P(),
        P(None, "coil", None, None),
    )
    return jax.shard_map(
        per_device,
        mesh=mesh,
        in_specs=placed,
        out_specs=P(None, "kz", "coil", None),
        check_vma=False,
    )
```

profile of v0, /device:TPU:1, one launch (start us, length us, event | category | flops | bytes accessed | tf_op | source)
XLA Modules:
  0.0 226.4 jit_solution(4837455804262960752)
XLA Ops:
  1.4 6.2 %convert_bitcast_fusion = bf16[2,16,64,512]{3,2,0,1:T(8,128)(2,1)} fusion(pred[256,64]{0,1:T(8,128)(4,1)S(1)} %iota_compare_fusion, pred[16,256]{1,0:T(8,128)(4,1)S(1)} %iota_compare_fusion.1, bf16[2,16,1,256,512]{4,3,2,1,0:T(8,128)(2,1)} %param.6), kind=kOutput, calls=%fused_computation.20 | convolution fusion | flops 538181632 | bytes 10506240 | tf_op jit(solution)/shard_map/rpsn,psa->rpan/dot_general | solution.py:64
  7.6 2.6 %reshape.99 = bf16[2,16,64,4,128]{4,3,2,0,1:T(4,128)(2,1)S(1)} reshape(bf16[2,16,64,512]{3,2,0,1:T(8,128)(2,1)} %convert_bitcast_fusion) | data formatting | bytes 4194304 | tf_op jit(solution)/shard_map/reshape | solution.py:71
  10.4 7.6 %fusion = f32[64,4,2,16,128]{4,3,2,1,0:T(8,128)} fusion(bf16[64,4,128,128]{3,2,1,0:T(8,128)(2,1)} %param.10, bf16[2,16,64,4,128]{4,3,2,0,1:T(4,128)(2,1)S(1)} %reshape.99), kind=kOutput, calls=%fused_computation.2 | convolution fusion | flops 268435456 | bytes 14680064 | tf_op jit(solution)/shard_map/rpagj,agjt->rpagt/dot_general | solution.py:72
  18.1 3.8 %broadcast_in_dim.4 = f32[2,16,512,128]{3,1,2,0:T(8,128)} broadcast(f32[]{:T(128)} %constant.43.clone.1), dimensions={} | broadcast | bytes 8388612 | tf_op jit(solution)/shard_map/broadcast_in_dim | solution.py:73
  21.8 34.6 %scatter_fusion = f32[2,16,512,128]{3,1,2,0:T(8,128)} fusion(f32[2,16,512,128]{3,1,2,0:T(8,128)} %broadcast_in_dim.4, s32[256]{0:T(256)S(1)} %bitcast.97, f32[256,2,16,128]{3,2,1,0:T(8,128)} %bitcast.91), kind=kCustom, calls=%fused_computation | custom fusion | flops 1048576 | bytes 12583936 | tf_op jit(solution)/shard_map/scatter-add | solution.py:74
  56.5 3.9 %convert_element_type.68 = bf16[2,16,512,128]{3,1,2,0:T(8,128)(2,1)S(1)} convert(f32[2,16,512,128]{3,1,2,0:T(8,128)} %scatter_fusion) | non-fusion elementwise | flops 2097152 | bytes 12582912 | tf_op jit(solution)/shard_map/convert_element_type | solution.py:75
  60.4 2.0 fusion.117
  62.4 1.9 copy.31
  64.3 2.7 %squeeze.11 = bf16[16,256,256]{2,1,0:T(8,128)(2,1)S(1)} reshape(bf16[1,16,512,128]{3,2,1,0:T(8,128)(2,1)} %copy.31) | data formatting | bytes 4194304 | tf_op jit(solution)/shard_map/squeeze | solution.py:76
  67.0 3.6 %fusion.35 = f32[16,256,256]{2,1,0:T(8,128)} fusion(bf16[16,256,256]{2,1,0:T(8,128)(2,1)S(1)} %squeeze.11), kind=kOutput, calls=%fused_computation.46 | convolution fusion | flops 537919488 | bytes 6291456 | tf_op jit(solution)/shard_map/ky,pyx->pkx/dot_general | solution.py:76
  70.6 1.9 copy.33
  72.5 4.1 %squeeze.12 = bf16[16,256,256]{2,1,0:T(8,128)(2,1)} reshape(bf16[1,16,512,128]{3,2,1,0:T(8,128)(2,1)} %copy.33) | data formatting | bytes 4194304 | tf_op jit(solution)/shard_map/squeeze | solution.py:77
  76.6 3.4 %fusion.32 = f32[16,256,256]{2,1,0:T(8,128)S(1)} fusion(bf16[16,256,256]{2,1,0:T(8,128)(2,1)} %squeeze.12), kind=kOutput, calls=%fused_computation.45 | convolution fusion | flops 537919488 | bytes 6291456 | tf_op jit(solution)/shard_map/ky,pyx->pkx/dot_general | solution.py:79
  80.0 1.7 add_convert_fusion
  81.7 1.7 subtract_convert_fusion
  83.4 1.7 fusion.4
  85.1 1.7 fusion.8
  86.8 1.7 convolution_subtract_fusion
  88.6 2.7 %add_bitcast_fusion = (f32[1,16,32,8,256]{4,3,2,1,0:T(8,128)S(1)}, f32[1,16,32,8,256]{4,3,2,1,0:T(8,128)S(1)}) fusion(f32[16,256,256]{2,1,0:T(8,128)S(1)} %convolution_subtract_fusion, f32[256,256]{1,0:T(8,128)S(1)} %get-tuple-element.12, f32[256,256]{1,0:T(8,128)S(1)} %get-tuple-element.11, f32[16,256,256]{2,1,0:T(8,128)S(1)} %fusion.8, ...), kind=kOutput, calls=%fused_computation.8 | convolution fusion | flops 545259520 | bytes 19398656 | tf_op jit(solution)/shard_map/pkx,mx->pkm/dot_general | solution.py:84
  92.3 103.8 %all_to_all.10 = f32[32,2,16,8,256]{4,3,2,1,0:T(8,128)} all-to-all(f32[32,2,16,8,256]{4,3,2,1,0:T(8,128)S(1)} %copy_bitcast_fusion), channel_id=1, replica_groups=mesh['coil'=32,'kz'=4] {'coil'}, dimensions={0} | all-to-all | bytes 16777216 | tf_op jit(solution)/shard_map/all_to_all | solution.py:15
  196.1 3.9 %reduce_sum.9 = f32[2,16,8,256]{3,2,1,0:T(8,128)S(1)} reduce(f32[32,2,16,8,256]{4,3,2,1,0:T(8,128)} %all_to_all.10, f32[]{:T(128)} %constant.43.clone.1), dimensions={0}, to_apply=%region_1.2 | reduce | flops 2031616 | bytes 8650756 | tf_op jit(solution)/shard_map/reduce_sum | solution.py:16
  200.2 1.1 broadcast_in_dim.5
  201.3 7.2 %all-to-all-start.1 = ((f32[4,2,16,8,256]{4,2,3,1,0:T(8,128)}), f32[4,2,16,8,256]{4,2,3,1,0:T(8,128)S(1)}, u32[]{:S(2)}, u32[]{:S(2)}) async-start(f32[4,2,16,8,256]{4,2,3,1,0:T(8,128)} %broadcast_in_dim.5), calls=%async_computation.1 | async-start | bytes 2097152 | tf_op jit(solution)/shard_map/all_to_all | solution.py:27
  208.5 15.0 %all-to-all-done.1 = f32[4,2,16,8,256]{4,2,3,1,0:T(8,128)S(1)} async-done(((f32[4,2,16,8,256]{4,2,3,1,0:T(8,128)}), f32[4,2,16,8,256]{4,2,3,1,0:T(8,128)S(1)}, u32[]{:S(2)}, u32[]{:S(2)}) %all-to-all-start.1) | async-done | bytes 1048608 | tf_op jit(solution)/shard_map/all_to_all | solution.py:27
  (29 shorter events, 5.7 us)
Async XLA Ops:
  7.6 2.6 %copy-start.4 = (s32[64,4]{0,1:T(4,128)S(1)}, s32[64,4]{0,1:T(4,128)}, u32[]{:S(2)}) copy-start(s32[64,4]{0,1:T(4,128)} %param.9) | copy-start | bytes 3076
  67.0 3.6 %copy-start.2 = (bf16[1,16,512,128]{3,1,2,0:T(8,128)(2,1)S(1)}, bf16[1,16,512,128]{3,1,2,0:T(8,128)(2,1)}, u32[]{:S(2)}) copy-start(bf16[1,16,512,128]{3,1,2,0:T(8,128)(2,1)} %get-tuple-element.7) | copy-start | bytes 6291460
  76.6 3.4 %copy-start = (bf16[16,256,256]{2,1,0:T(8,128)(2,1)S(1)}, bf16[16,256,256]{2,1,0:T(8,128)(2,1)}, u32[]{:S(2)}) copy-start(bf16[16,256,256]{2,1,0:T(8,128)(2,1)} %squeeze.12) | copy-start | bytes 6291460
  76.6 3.5 %copy-start.1 = (f32[16,256,256]{2,1,0:T(8,128)S(1)}, f32[16,256,256]{2,1,0:T(8,128)}, u32[]{:S(2)}) copy-start(f32[16,256,256]{2,1,0:T(8,128)} %fusion.35) | copy-start | bytes 12582916
  86.8 1.7 copy-start.3
  201.3 22.2 %all-to-all-start.1 = ((f32[4,2,16,8,256]{4,2,3,1,0:T(8,128)}), f32[4,2,16,8,256]{4,2,3,1,0:T(8,128)S(1)}, u32[]{:S(2)}, u32[]{:S(2)}) async-start(f32[4,2,16,8,256]{4,2,3,1,0:T(8,128)} %broadcast_in_dim.5), calls=%async_computation.1 | async-start | bytes 2097152 | tf_op jit(solution)/shard_map/all_to_all | solution.py:27
where the time goes:
time: 227 us; the launch traced here: 226 us
  blocking collectives  104 us (46%)
  other arithmetic  45 us (20%)
  matrix products  33.8 us (15%)
  local copies, waits for them, and re-layouts  21.4 us (9%)
  waiting for transfers between devices  15 us (7%)
  starting transfers between devices  7.21 us (3%)
    all_to_all x1, blocking collectives, sum_at_owner(): lax.all_to_all(tiles, axis, split_axis=0, concat_axis=0, tiled=True)  104 us
    scatter-add x1, other arithmetic, coil_image(): flat.at[:, :, block_index.reshape(-1)]  34.6 us
    all_to_all x1, waiting for transfers between devices, from_everyone(): return lax.all_to_all(copies, axis, split_axis=0, concat_axis=0, tiled=True)  15 us
    dot_general x1, matrix products, coil_image(): jnp.einsum('rpagj,agjt->rpagt', pieces, interp, preferred_element_type=f32)  7.64 us
    all_to_all x1, starting transfers between devices, from_everyone(): return lax.all_to_all(copies, axis, split_axis=0, concat_axis=0, tiled=True)  7.21 us
    dot_general x1, matrix products, coil_image(): jnp.einsum('rpsn,psa->rpan', data, weights, preferred_element_type=f32)  6.2 us
  transfers between devices with their start and end apart: 1, of which 1 were waited for; matrix products, arithmetic and copies ran while one was open for 0% of the time, Pallas kernels for 0%

commit v1 on v0

--- a/solution.py
+++ b/solution.py
@@ -69,18 +69,22 @@
     gdim = mdim // seg
     side = cos_t.shape[0]
     pieces = binned.reshape(rdim, pdim, adim, gdim, seg)
-    contrib = jnp.einsum("rpagj,agjt->rpagt", pieces, interp, preferred_element_type=f32)
-    flat = jnp.zeros((rdim, pdim, side * side // seg, seg), f32)
-    flat = flat.at[:, :, block_index.reshape(-1)].add(contrib.reshape(rdim, pdim, adim * gdim, seg))
-    grid = flat.reshape(rdim, pdim, side, side).astype(jnp.bfloat16)
-    half_re = jnp.einsum("ky,pyx->pkx", cos_t, grid[0], preferred_element_type=f32) + jnp.einsum(
-        "ky,pyx->pkx", sin_t, grid[1], preferred_element_type=f32
+    contrib = jnp.einsum("rpagj,agjt->agrpt", pieces, interp, preferred_element_type=f32).astype(jnp.bfloat16)
+    contrib = contrib.reshape(adim * gdim, rdim, pdim, seg)
+    xdim = side // seg
+    blocks = block_index.reshape(-1)
+    spread = (blocks[None, :] == jnp.arange(side * xdim, dtype=jnp.int32)[:, None]).astype(jnp.bfloat16)
+    spread = spread.reshape(side, xdim, adim * gdim)
+    cos_g = jnp.einsum("ky,yhq->hkq", cos_t, spread, preferred_element_type=f32).astype(jnp.bfloat16)
+    sin_g = jnp.einsum("ky,yhq->hkq", sin_t, spread, preferred_element_type=f32).astype(jnp.bfloat16)
+    half_re = jnp.einsum("hkq,qpt->pkht", cos_g, contrib[:, 0], preferred_element_type=f32) + jnp.einsum(
+        "hkq,qpt->pkht", sin_g, contrib[:, 1], preferred_element_type=f32
     )
-    half_im = jnp.einsum("ky,pyx->pkx", cos_t, grid[1], preferred_element_type=f32) - jnp.einsum(
-        "ky,pyx->pkx", sin_t, grid[0], preferred_element_type=f32
+    half_im = jnp.einsum("hkq,qpt->pkht", cos_g, contrib[:, 1], preferred_element_type=f32) - jnp.einsum(
+        "hkq,qpt->pkht", sin_g, contrib[:, 0], preferred_element_type=f32
     )
-    half_re = half_re.astype(jnp.bfloat16)
-    half_im = half_im.astype(jnp.bfloat16)
+    half_re = half_re.astype(jnp.bfloat16).reshape(pdim, side, side)
+    half_im = half_im.astype(jnp.bfloat16).reshape(pdim, side, side)
     out_re = jnp.einsum("pkx,mx->pkm", half_re, cos_t, preferred_element_type=f32) + jnp.einsum(
         "pkx,mx->pkm", half_im, sin_t, preferred_element_type=f32
     )
@@ -110,7 +114,7 @@
     image_c = coil_image(data, weights, interp, block_index, cos_t, sin_t)
     sens_here = sens_maps.astype(jnp.float32)
     weighted = conj_product(sens_here[:, 0][:, None], image_c)
-    combined = sum_at_owner(weighted, "coil", 2)
+    combined = lax.psum_scatter(weighted, "coil", scatter_dimension=2, tiled=True)
     groups = lax.axis_size("kz")
     kz_total = parts_here * groups
     my_first = lax.axis_index("kz") * parts_here

time: 227 us -> 266 us (1.17)
  waiting for transfers between devices: 15 us -> 206 us
  blocking collectives: 104 us -> 0 us
  other arithmetic: 45 us -> 5.28 us
  between operations: 0.22 us -> 13.6 us
  local copies, waits for them, and re-layouts: 21.4 us -> 8.32 us
  matrix products: 33.8 us -> 26.6 us
    reduce_scatter x0 -> x1, waiting for transfers between devices: none -> 191 us  [per_device(): lax.psum_scatter(weighted, 'coil', scatter_dimension=2, tiled=True)]
    all_to_all x1 -> x0, blocking collectives: 104 us -> none  [sum_at_owner(): lax.all_to_all(tiles, axis, split_axis=0, concat_axis=0, tiled=True)]
    scatter-add x1 -> x0, other arithmetic: 34.6 us -> none  [coil_image(): flat.at[:, :, block_index.reshape(-1)]]
    squeeze x2 -> x0, local copies, waits for them, and re-layouts: 6.78 us -> none  [the longest x1 4.11 us: coil_image(): grid[1]]
    dot_general x5 -> x7, matrix products: 18 us -> 12.4 us  [the longest x1 6.31 us: coil_image(): jnp.einsum('rpagj,agjt->agrpt', pieces, interp, preferred_element_type=f32)]
    slice x3 -> x1, local copies, waits for them, and re-layouts: 5.78 us -> 0.38 us  [coil_image(): contrib[:, 1]]
    reduce_sum x1 -> x0, other arithmetic: 3.94 us -> none  [sum_at_owner(): return arrived.sum(axis=0)]
    convert_element_type x1 -> x0, other arithmetic: 3.92 us -> none  [coil_image(): grid = flat.reshape(rdim, pdim, side, side).astype(jnp.bfloat16)]
  transfers between devices with their start and end apart: 1 -> 2, of which waited for: 1 -> 2; matrix products, arithmetic and copies ran while one was open for 0% -> 0% of each run, Pallas kernels for 0% -> 0%
where the time goes in v1:
time: 266 us
  waiting for transfers between devices  206 us (77%)
  matrix products  26.6 us (10%)
  between operations  13.6 us (5%)
  local copies, waits for them, and re-layouts  8.32 us (3%)
  starting transfers between devices  6.13 us (2%)
  other arithmetic  5.28 us (2%)
    reduce_scatter x1, waiting for transfers between devices, per_device(): lax.psum_scatter(weighted, 'coil', scatter_dimension=2, tiled=True)  191 us
    all_to_all x1, waiting for transfers between devices, from_everyone(): return lax.all_to_all(copies, axis, split_axis=0, concat_axis=0, tiled=True)  15 us
    dot_general x1, matrix products, coil_image(): jnp.einsum('rpagj,agjt->agrpt', pieces, interp, preferred_element_type=f32)  6.31 us
    all_to_all x1, starting transfers between devices, from_everyone(): return lax.all_to_all(copies, axis, split_axis=0, concat_axis=0, tiled=True)  6.13 us
  transfers between devices with their start and end apart: 2, of which 2 were waited for; matrix products, arithmetic and copies ran while one was open for 0% of the time, Pallas kernels for 0%

profile of v1, /device:TPU:1, one launch (start us, length us, event | category | flops | bytes accessed | tf_op | source)
XLA Modules:
  0.0 266.1 jit_solution(2261909338097157264)
XLA Ops:
  6.5 0.8 copy.39
  7.4 1.2 fusion.12
  8.6 1.9 fusion.13
  11.2 0.7 iota_compare_fusion.1
  11.9 4.9 %convert_bitcast_fusion = bf16[2,16,64,512]{3,2,0,1:T(8,128)(2,1)S(1)} fusion(pred[256,64]{0,1:T(8,128)(4,1)S(1)} %iota_compare_fusion, pred[16,256]{1,0:T(8,128)(4,1)S(1)} %iota_compare_fusion.1, bf16[2,16,1,256,512]{4,3,2,1,0:T(8,128)(2,1)} %param.6), kind=kOutput, calls=%fused_computation.12 | convolution fusion | flops 538181632 | bytes 10506240 | tf_op jit(solution)/shard_map/rpsn,psa->rpan/dot_general | solution.py:64
  16.8 2.1 reshape.78
  18.9 6.3 %fusion.7 = bf16[64,4,2,16,128]{4,3,2,1,0:T(8,128)(2,1)S(1)} fusion(bf16[64,4,128,128]{3,2,1,0:T(8,128)(2,1)} %param.10, bf16[2,16,64,4,128]{4,3,2,0,1:T(4,128)(2,1)} %reshape.78), kind=kOutput, calls=%fused_computation.13 | convolution fusion | flops 269484032 | bytes 12582912 | tf_op jit(solution)/shard_map/rpagj,agjt->agrpt/dot_general | solution.py:72
  25.6 0.8 copy.69
  26.4 1.0 copy.70
  27.4 0.7 fusion.17
  28.1 0.7 fusion.19
  28.8 0.8 add_convert_fusion
  29.6 0.8 subtract_convert_fusion
  30.4 1.7 fusion.43
  32.1 1.7 fusion.45
  33.7 1.7 convolution_subtract_fusion
  35.5 2.5 add_bitcast_fusion
  38.1 3.8 %pad_maximum_fusion = f32[2,16,256,256]{3,2,1,0:T(8,128)} fusion(f32[1,16,256,256]{3,2,1,0:T(8,128)S(1)} %get-tuple-element.6, f32[1,16,256,256]{3,2,1,0:T(8,128)S(1)} %get-tuple-element.5), kind=kLoop, calls=%fused_computation | loop fusion | flops 2097152 | bytes 16777216 | tf_op jit(solution)/shard_map/stack | solution.py:100
  41.9 191.3 %reduce-scatter.2.cloned.1.call-done = f32[2,16,8,256]{3,2,1,0:T(8,128)} async-done(((f32[2,16,256,256]{3,2,1,0:T(8,128)}), f32[2,16,8,256]{3,2,1,0:T(8,128)}) %reduce-scatter.2.cloned.1.call-update) | async-done | bytes 262160 | tf_op jit(solution)/shard_map/reduce_scatter | solution.py:117
  233.1 1.0 copy.49
  234.2 1.1 broadcast_in_dim.2
  235.3 6.1 %all-to-all-start = ((f32[4,2,16,8,256]{4,2,3,1,0:T(8,128)}), f32[4,2,16,8,256]{4,2,3,1,0:T(8,128)S(1)}, u32[]{:S(2)}, u32[]{:S(2)}) async-start(f32[4,2,16,8,256]{4,2,3,1,0:T(8,128)} %broadcast_in_dim.2), calls=%async_computation.1 | async-start | bytes 2097152 | tf_op jit(solution)/shard_map/all_to_all | solution.py:27
  241.4 15.0 %all-to-all-done = f32[4,2,16,8,256]{4,2,3,1,0:T(8,128)S(1)} async-done(((f32[4,2,16,8,256]{4,2,3,1,0:T(8,128)}), f32[4,2,16,8,256]{4,2,3,1,0:T(8,128)S(1)}, u32[]{:S(2)}, u32[]{:S(2)}) %all-to-all-start) | async-done | bytes 1048608 | tf_op jit(solution)/shard_map/all_to_all | solution.py:27
  258.4 0.9 copy.52
  (21 shorter events, 3.3 us)
Async XLA Ops:
  6.5 226.6 %reduce-scatter.2.cloned.1.call-start = ((), (), s32[]{:S(2)}) async-start(), calls=%async_computation.2 | async-start | bytes 8650752 | tf_op jit(solution)/shard_map/reduce_scatter | solution.py:117
  27.4 1.4 copy-start
  33.7 1.7 copy-start.1
  235.3 21.1 %all-to-all-start = ((f32[4,2,16,8,256]{4,2,3,1,0:T(8,128)}), f32[4,2,16,8,256]{4,2,3,1,0:T(8,128)S(1)}, u32[]{:S(2)}, u32[]{:S(2)}) async-start(f32[4,2,16,8,256]{4,2,3,1,0:T(8,128)} %broadcast_in_dim.2), calls=%async_computation.1 | async-start | bytes 2097152 | tf_op jit(solution)/shard_map/all_to_all | solution.py:27
Sparse Core Ops, SparseCore 0:
  42.0 191.1 reduce-scatter.1

commit v2 on v0

v2 whole, which is shorter than its diff:
```python
import functools

import jax
import jax.numpy as jnp
import numpy as np
from jax import lax
from jax.experimental import pallas as pl
from jax.experimental.pallas import tpu as pltpu
from jax.sharding import PartitionSpec as P

F32 = jnp.float32
BF16 = jnp.bfloat16
MESH = pl.DeviceIdType.MESH

PPC = 2
BPAD = 40
LAGS = (0, 2, 4, 6, 8, 10)

STREAMS = ((True, 1), (True, 3), (False, 1), (False, 3))


def dft_np(rows, cols, length):
    product = (rows[:, None] * cols[None, :]) % length
    phase = product.astype(np.float64) * (2.0 * np.pi / length)
    return np.cos(phase) / np.sqrt(length), np.sin(phase) / np.sqrt(length)


def plane_table(side):
    index = np.arange(side)
    cos_t, sin_t = dft_np(index, index, side)
    table = np.block([[cos_t, -sin_t], [sin_t, cos_t]])
    return jnp.asarray(table, dtype=BF16)


def kz_table(groups, parts):
    total = groups * parts
    index = np.arange(total)
    cos_z, sin_z = dft_np(index, index, total)
    blocks = []
    for g in range(groups):
        c = cos_z[g * parts : (g + 1) * parts].reshape(parts, groups, 1, parts)
        s = sin_z[g * parts : (g + 1) * parts].reshape(parts, groups, 1, parts)
        real = np.concatenate([c, s], axis=2).reshape(parts, -1)
        imag = np.concatenate([-s, c], axis=2).reshape(parts, -1)
        blocks.append(np.concatenate([real, imag], axis=0))
    return jnp.asarray(np.stack(blocks), dtype=F32)


def flip(i, pairing):
    return i + 1 - 2 * (i % 2) if pairing == 1 else 3 - i


def kernel(
    parts, angles, spokes, side,
    count_ref, angle_ref, block_ref, ztab_ref,
    kdata_hbm, interp_hbm, sens_hbm, plane_hbm,
    out_ref,
    kd, itp, sens_v, plane, tab, sensp, binned, spread, half,
    img, r1x, r1y, r2, r3, r4, r5, gath, kzout,
    load_sem, send_sem, recv_sem, kz_send, kz_recv,
):
    chunks = parts // PPC
    segs = 4
    seg = 128
    hits = angles * segs
    xpad = hits + 8
    coil = lax.axis_index("coil")
    group = lax.axis_index("kz")
    x, y, z = coil // 8, (coil // 2) % 4, coil % 2

    def dev(axis_x, pairing):
        if axis_x:
            return ((flip(x, pairing) * 4 + y) * 2 + z, group)
        return ((x * 4 + flip(y, pairing)) * 2 + z, group)

    zdev = ((x * 4 + y) * 2 + 1 - z, group)
    kzdevs = [(coil, (group + d) % 4) for d in range(1, 4)]

    loads = [
        pltpu.make_async_copy(plane_hbm, plane, load_sem.at[0]),
        pltpu.make_async_copy(sens_hbm, sens_v, load_sem.at[1]),
    ]
    kloads = [
        pltpu.make_async_copy(
            kdata_hbm.at[:, pl.ds(q * (parts // 4), parts // 4)],
            kd.at[:, pl.ds(q * (parts // 4), parts // 4)],
            load_sem.at[2 + q],
        )
        for q in range(4)
    ]
    iloads = [
        pltpu.make_async_copy(
            interp_hbm.at[pl.ds(q * (angles // 4), angles // 4)],
            itp.at[pl.ds(q * (angles // 4), angles // 4)],
            load_sem.at[6 + q],
        )
        for q in range(4)
    ]
    for copy in loads + kloads + iloads:
        copy.start()

    barrier = pltpu.get_barrier_semaphore()
    peers = [dev(a, p) for a in (True, False) for p in (1, 3)] + [zdev] + kzdevs
    for peer in peers:
        pl.semaphore_signal(barrier, inc=1, device_id=peer, device_id_type=MESH)

    for copy in loads:
        copy.wait()
    row = lax.broadcasted_iota(jnp.int32, (side, side), 0)
    col = lax.broadcasted_iota(jnp.int32, (side, side), 1)
    perm = jnp.where(jnp.bitwise_xor(row, col) == coil * 8, 1.0, 0.0).astype(BF16)
    cos_p = jnp.dot(perm, plane[0:side, 0:side], preferred_element_type=F32).astype(BF16)
    sin_p = jnp.dot(perm, plane[side : 2 * side, 0:side], preferred_element_type=F32).astype(BF16)
    blocks = jnp.broadcast_to(block_ref[0:1, :], (side, hits))
    yrow = lax.broadcasted_iota(jnp.int32, (side, hits), 0)
    for h in range(2):
        onto = jnp.where(blocks == yrow * 2 + h, 1.0, 0.0).astype(BF16)
        cos_g = jnp.dot(cos_p, onto, preferred_element_type=F32)
        sin_g = jnp.dot(sin_p, onto, preferred_element_type=F32)
        tab[h, 0:side, 0:hits] = cos_g.astype(BF16)
        tab[h, side : 2 * side, hits : 2 * hits] = cos_g.astype(BF16)
        tab[h, 0:side, hits : 2 * hits] = sin_g.astype(BF16)
        tab[h, side : 2 * side, 0:hits] = (-sin_g).astype(BF16)
    for r in range(2):
        sensp[r] = jnp.dot(perm, sens_v[r], preferred_element_type=F32)

    arow = lax.broadcasted_iota(jnp.int32, (angles, spokes), 0)
    scol = lax.broadcasted_iota(jnp.int32, (angles, spokes), 1)
    match = jnp.broadcast_to(angle_ref[0:1, :], (angles, spokes)) == arow
    for q in range(4):
        kloads[q].wait()

        def bin_one(i, carry):
            p = q * (parts // 4) + i
            used = jnp.logical_and(match, scol < count_ref[p])
            weights = jnp.where(used, 1.0, 0.0).astype(BF16)
            for r in range(2):
                summed = jnp.dot(weights, kd[r, p], preferred_element_type=F32)
                for g in range(segs):
                    start = g * angles * BPAD + r * parts + p
                    binned[pl.ds(start, angles, stride=BPAD), :] = summed[:, g * seg : (g + 1) * seg]
            return carry

        lax.fori_loop(0, parts // 4, bin_one, 0)

    batch = 4
    for q in range(4):
        iloads[q].wait()

        def spread_some(i, carry):
            for k in range(batch):
                a = q * (angles // 4) + i * batch + k
                for g in range(segs):
                    start = pl.multiple_of(g * angles * BPAD + a * BPAD, 8)
                    piece = binned[pl.ds(start, 2 * parts), :].astype(BF16)
                    got = jnp.dot(piece, itp[a, g], preferred_element_type=F32)
                    spread[pl.ds(a * segs + g, 2 * parts, stride=xpad), :] = got
            return carry

        lax.fori_loop(0, angles // 4 // batch, spread_some, 0)

    pl.semaphore_wait(barrier, len(peers))

    def make(c):
        ps = [c * PPC + k for k in range(PPC)]
        rows = []
        for r in range(2):
            pieces = [
                spread[pl.ds(pl.multiple_of((r * parts + p) * xpad, 8), hits), :].astype(BF16) for p in ps
            ]
            rows.append(jnp.concatenate(pieces, axis=1))
        stacked = jnp.concatenate(rows, axis=0)
        for h in range(2):
            got = jnp.dot(tab[h], stacked, preferred_element_type=F32).astype(BF16)
            for k in range(PPC):
                for r in range(2):
                    half[k, :, r * side + h * seg : r * side + (h + 1) * seg] = got[
                        r * side : (r + 1) * side, k * seg : (k + 1) * seg
                    ]
        for k in range(PPC):
            full = jnp.dot(half[k], plane[...], preferred_element_type=F32)
            s_re, s_im = sensp[0], sensp[1]
            o_re, o_im = full[:, 0:side], full[:, side : 2 * side]
            w_re = s_re * o_re + s_im * o_im
            w_im = s_re * o_im - s_im * o_re
            for h in range(2):
                cols = slice(h * seg, (h + 1) * seg)
                img[h, ps[k]] = w_re[:, cols].reshape(4, 4, 16, seg)
                img[2 + h, ps[k]] = w_im[:, cols].reshape(4, 4, 16, seg)

    def slots(pairing):
        return (1, 0, 1, 3) if pairing == 1 else (2, 1, 0, 1)

    def copies(s, stage, ps):
        first_x, pairing = STREAMS[s]
        sent, keep, onward, quarter = slots(pairing)
        if stage == 1:
            peer = dev(first_x, pairing)
            if first_x:
                src, dst = img.at[s, ps, pl.ds(sent, 2)], r1x.at[s, ps]
            else:
                src, dst = img.at[s, ps, :, pl.ds(sent, 2)], r1y.at[s - 2, ps]
        elif stage == 2:
            peer = dev(first_x, 4 - pairing)
            src = r1x.at[s, ps, onward] if first_x else r1y.at[s - 2, ps, :, onward]
            dst = r2.at[s, ps]
        elif stage == 3:
            peer = dev(not first_x, pairing)
            src, dst = r2.at[s, ps, pl.ds(sent, 2)], r3.at[s, ps]
        elif stage == 4:
            peer = dev(not first_x, 4 - pairing)
            src, dst = r3.at[s, ps, onward], r4.at[s, ps]
        else:
            peer = zdev
            src, dst = r4.at[s, ps, pl.ds(8, 8)], r5.at[s, ps]
        return src, dst, peer

    def remote(s, stage, c):
        src, dst, peer = copies(s, stage, pl.ds(c * PPC, PPC))
        return pltpu.make_async_remote_copy(
            src_ref=src, dst_ref=dst,
            send_sem=send_sem.at[stage - 1, s], recv_sem=recv_sem.at[stage - 1, s, c],
            device_id=peer, device_id_type=MESH,
        )

    def held(s, ps, quarters, rows=slice(None)):
        first_x, pairing = STREAMS[s]
        keep = slots(pairing)[1]
        if first_x:
            return img[s, ps, 0, quarters, rows] + r1x[s, ps, keep, quarters, rows] + r2[s, ps, quarters, rows]
        return img[s, ps, quarters, 0, rows] + r1y[s - 2, ps, quarters, keep, rows] + r2[s, ps, quarters, rows]

    def step(stage, c):
        ps = pl.ds(c * PPC, PPC)
        for s in range(4):
            first_x, pairing = STREAMS[s]
            sent, keep, onward, quarter = slots(pairing)
            if stage > 1:
                remote(s, stage - 1, c).wait_recv()
            if stage == 2:
                if first_x:
                    r1x[s, ps, onward] += img[s, ps, quarter]
                else:
                    r1y[s - 2, ps, :, onward] += img[s, ps, :, quarter]
            elif stage == 3:
                r2[s, ps, sent : sent + 2] = held(s, ps, slice(sent, sent + 2))
            elif stage == 4:
                r3[s, ps, onward] += held(s, ps, quarter)
            elif stage == 5:
                rows = slice(8, 16)
                r4[s, ps, rows] += held(s, ps, 0, rows) + r3[s, ps, keep, rows]
            elif stage == 6:
                rows = slice(0, 8)
                gath[group, s, ps] = held(s, ps, 0, rows) + r3[s, ps, keep, rows] + r4[s, ps, rows] + r5[s, ps]
            if stage < 6:
                remote(s, stage, c).start()

    def kz_remote(d, c, slot):
        ps = pl.ds(c * PPC, PPC)
        return pltpu.make_async_remote_copy(
            src_ref=gath.at[slot, :, ps], dst_ref=gath.at[slot, :, ps],
            send_sem=kz_send.at[d], recv_sem=kz_recv.at[slot, c],
            device_id=kzdevs[d], device_id_type=MESH,
        )

    def pipeline(i, carry):
        @pl.when(i < chunks)
        def _():
            make(i)
            step(1, i)

        for stage in range(2, 7):
            c = i - LAGS[stage - 1]

            @pl.when(jnp.logical_and(c >= 0, c < chunks))
            def _():
                step(stage, c)
                if stage == 6:
                    for d in range(3):
                        kz_remote(d, c, group).start()

        return carry

    lax.fori_loop(0, chunks + LAGS[5], pipeline, 0)

    for d in range(3):
        for c in range(chunks):
            kz_remote(d, c, (group + d + 1) % 4).wait_recv()

    for mh in range(2):
        for yy in range(8):
            pieces = []
            for g in range(4):
                for r in range(2):
                    pieces.append(gath[g, r * 2 + mh, :, yy, :])
            stacked = jnp.concatenate(pieces, axis=0)
            got = jnp.dot(ztab_ref[group], stacked, preferred_element_type=F32, precision=lax.Precision.HIGHEST)
            kzout[mh, pl.ds(yy, 2 * parts, stride=8), :] = got
        out_ref[:, :, :, mh * seg : (mh + 1) * seg] = kzout[mh].reshape(2, parts, 8, seg)

    everything = pl.ds(0, parts)
    for s in range(4):
        for stage in range(1, 6):
            src, dst, peer = copies(s, stage, everything)
            pltpu.make_async_remote_copy(
                src_ref=src, dst_ref=dst, send_sem=send_sem.at[stage - 1, s],
                recv_sem=recv_sem.at[stage - 1, s, 0], device_id=peer, device_id_type=MESH,
            ).wait_send()
    for d in range(3):
        pltpu.make_async_remote_copy(
            src_ref=gath.at[group], dst_ref=gath.at[group], send_sem=kz_send.at[d],
            recv_sem=kz_recv.at[group, 0], device_id=kzdevs[d], device_id_type=MESH,
        ).wait_send()


def per_device(kdata, spoke_angle, spoke_count, block_index, interp, sens_maps):
    side = sens_maps.shape[2]
    parts = kdata.shape[1]
    spokes, samples = kdata.shape[3], kdata.shape[4]
    angles, segs, seg = interp.shape[0], interp.shape[1], interp.shape[2]
    hits = angles * segs
    chunks = parts // PPC
    any_spec = pl.BlockSpec(memory_space=pl.ANY)
    vmem_spec = pl.BlockSpec(memory_space=pltpu.VMEM)
    return pl.pallas_call(
        functools.partial(kernel, parts, angles, spokes, side),
        out_shape=jax.ShapeDtypeStruct((2, parts, 8, side), F32),
        in_specs=[pl.BlockSpec(memory_space=pltpu.SMEM)] + [vmem_spec] * 3 + [any_spec] * 4,
        out_specs=vmem_spec,
        scratch_shapes=[
            pltpu.VMEM((2, parts, spokes, samples), BF16),
            pltpu.VMEM((angles, segs, seg, seg), BF16),
            pltpu.VMEM((2, side, side), BF16),
            pltpu.VMEM((2 * side, 2 * side), BF16),
            pltpu.VMEM((2, 2 * side, 2 * hits), BF16),
            pltpu.VMEM((2, side, side), F32),
            pltpu.VMEM((segs * angles * BPAD, seg), F32),
            pltpu.VMEM((2 * parts * (hits + 8), seg), F32),
            pltpu.VMEM((PPC, side, 2 * side), BF16),
            pltpu.VMEM((4, parts, 4, 4, 16, seg), F32),
            pltpu.VMEM((2, parts, 2, 4, 16, seg), F32),
            pltpu.VMEM((2, parts, 4, 2, 16, seg), F32),
            pltpu.VMEM((4, parts, 4, 16, seg), F32),
            pltpu.VMEM((4, parts, 2, 16, seg), F32),
            pltpu.VMEM((4, parts, 16, seg), F32),
            pltpu.VMEM((4, parts, 8, seg), F32),
            pltpu.VMEM((4, 4, parts, 8, seg), F32),
            pltpu.VMEM((2, 2 * parts * 8, seg), F32),
            pltpu.SemaphoreType.DMA((10,)),
            pltpu.SemaphoreType.DMA((5, 4)),
            pltpu.SemaphoreType.DMA((5, 4, chunks)),
            pltpu.SemaphoreType.DMA((3,)),
            pltpu.SemaphoreType.DMA((4, chunks)),
        ],
        compiler_params=pltpu.CompilerParams(
            collective_id=0, has_side_effects=True, vmem_limit_bytes=63 << 20
        ),
    )(
        spoke_count,
        spoke_angle.reshape(1, spokes),
        block_index.reshape(1, hits),
        kz_table(4, parts),
        kdata[:, :, 0],
        interp,
        sens_maps[:, 0],
        plane_table(side),
    )


def solution(mesh):
    placed = (
        P(None, "kz", "coil", None, None),
        P(),
        P("kz"),
        P(),
        P(),
        P(None, "coil", None, None),
    )
    return jax.shard_map(
        per_device,
        mesh=mesh,
        in_specs=placed,
        out_specs=P(None, "kz", "coil", None),
        check_vma=False,
    )
```

time: 227 us -> 81.1 us (0.36)
  blocking collectives: 104 us -> 0 us
  Pallas kernels: 0 us -> 77.8 us
  other arithmetic: 45 us -> 0 us
  matrix products: 33.8 us -> 0 us
  local copies, waits for them, and re-layouts: 21.4 us -> 3.11 us
  waiting for transfers between devices: 15 us -> 0 us
  starting transfers between devices: 7.21 us -> 0 us
    all_to_all x1 -> x0, blocking collectives: 104 us -> none  [sum_at_owner(): lax.all_to_all(tiles, axis, split_axis=0, concat_axis=0, tiled=True)]
    pallas_call x0 -> x1, Pallas kernels: none -> 77.8 us  [per_device(): pl.pallas_call(functools.partial(kernel, parts, angles, spokes, side), ou...]
    scatter-add x1 -> x0, other arithmetic: 34.6 us -> none  [coil_image(): flat.at[:, :, block_index.reshape(-1)]]
    dot_general x14 -> x0, matrix products: 33.8 us -> none  [the longest x1 7.64 us: coil_image(): jnp.einsum('rpagj,agjt->rpagt', pieces, interp, preferred_element_type=f32)]
    all_to_all x1 -> x0, waiting for transfers between devices: 15 us -> none  [from_everyone(): return lax.all_to_all(copies, axis, split_axis=0, concat_axis=0, tiled=True)]
    all_to_all x1 -> x0, starting transfers between devices: 7.21 us -> none  [from_everyone(): return lax.all_to_all(copies, axis, split_axis=0, concat_axis=0, tiled=True)]
    squeeze x2 -> x0, local copies, waits for them, and re-layouts: 6.78 us -> none  [the longest x1 4.11 us: coil_image(): grid[1]]
    slice x6 -> x0, local copies, waits for them, and re-layouts: 5.96 us -> none  [the longest x2 3.9 us: coil_image(): grid[1]]
  transfers between devices with their start and end apart: 1 -> 0, of which waited for: 1 -> 0; matrix products, arithmetic and copies ran while one was open for 0% -> 0% of each run, Pallas kernels for 0% -> 0%
where the time goes in v2:
time: 81.1 us; the launch traced here: 80.9 us
  Pallas kernels  77.8 us (96%)
  local copies, waits for them, and re-layouts  3.11 us (4%)
    pallas_call x1, Pallas kernels, per_device(): pl.pallas_call(functools.partial(kernel, parts, angles, spokes, side), ou...  77.8 us
    unnamed x2, local copies, waits for them, and re-layouts  2.44 us

profile of v2, /device:TPU:1, one launch (start us, length us, event | category | flops | bytes accessed | tf_op | source)
XLA Modules:
  0.0 80.9 jit_solution(17725333560761999805)
XLA Ops:
  0.0 0.8 copy.10
  0.8 0.7 reshape.7.block_ref
  1.4 77.8 %shard_map.82 = f32[2,16,8,256]{3,2,1,0:T(8,128)} custom-call(s32[16]{0:T(128)} %count_ref.1, s32[1,256]{1,0:T(1,128)} %bitcast.5, s32[1,256]{1,0:T(1,128)} %reshape.7.block_ref, f32[4,32,128]{2,1,0:T(8,128)} %constant.4.clone.ztab_ref, bf16[2,16,256,512]{3,2,1,0:T(8,128)(2,1)} %bitcast.3, bf16[64,4,128,128]{3,2,1,0:T(8,128)(2,1)} %interp_hbm.1, ...), custom_call_target="tpu_custom_call" | custom-call | tf_op jit(solution)/shard_map/pallas_call | solution.py:325
  79.2 1.7 %copy.12 = f32[2,16,8,256]{3,2,1,0:T(8,128)} copy(f32[2,16,8,256]{3,2,1,0:T(8,128)} %shard_map.82) | data formatting | bytes 524288

commit v3 on v2

v3 whole, which is shorter than its diff:
```python
import functools

import jax
import jax.numpy as jnp
import numpy as np
from jax import lax
from jax.experimental import pallas as pl
from jax.experimental.pallas import tpu as pltpu
from jax.sharding import PartitionSpec as P

F32 = jnp.float32
BF16 = jnp.bfloat16
MESH = pl.DeviceIdType.MESH

BPAD = 40

STREAMS = ((True, 1), (True, 3), (False, 1), (False, 3))


def dft_np(rows, cols, length):
    product = (rows[:, None] * cols[None, :]) % length
    phase = product.astype(np.float64) * (2.0 * np.pi / length)
    return np.cos(phase) / np.sqrt(length), np.sin(phase) / np.sqrt(length)


def plane_table(side):
    index = np.arange(side)
    cos_t, sin_t = dft_np(index, index, side)
    table = np.block([[cos_t, -sin_t], [sin_t, cos_t]])
    return jnp.asarray(table, dtype=BF16)


def kz_table(groups, parts):
    total = groups * parts
    index = np.arange(total)
    cos_z, sin_z = dft_np(index, index, total)
    blocks = []
    for g in range(groups):
        c = cos_z[g * parts : (g + 1) * parts].reshape(parts, groups, 1, parts)
        s = sin_z[g * parts : (g + 1) * parts].reshape(parts, groups, 1, parts)
        real = np.concatenate([c, s], axis=2).reshape(parts, -1)
        imag = np.concatenate([-s, c], axis=2).reshape(parts, -1)
        blocks.append(np.concatenate([real, imag], axis=0))
    return jnp.asarray(np.stack(blocks), dtype=F32)


def flip(i, pairing):
    return i + 1 - 2 * (i % 2) if pairing == 1 else 3 - i


def kernel(
    parts, angles, spokes, side,
    count_ref, angle_ref, block_ref, ztab_ref,
    kdata_hbm, interp_hbm, sens_hbm, plane_hbm,
    out_ref,
    kd, itp, sens_v, plane, tab, sensp, senso, binned, spread, other, half,
    img, r2x, r2y, r3, r4, r5, gath, kzout,
    load_sem, sens_send, sens_recv, send_sem, seg_recv, recv_sem, own_send, own_recv, kz_send, kz_recv,
):
    segs = 4
    seg = 128
    hits = angles * segs
    xpad = hits + 8
    coil = lax.axis_index("coil")
    group = lax.axis_index("kz")
    core = group % 2
    x, y, z = coil // 8, (coil // 2) % 4, coil % 2

    def dev(axis_x, pairing, over_z=False):
        zz = 1 - z if over_z else z
        if axis_x:
            return ((flip(x, pairing) * 4 + y) * 2 + zz, group)
        return ((x * 4 + flip(y, pairing)) * 2 + zz, group)

    zdev = ((x * 4 + y) * 2 + 1 - z, group)
    kzdevs = [(coil, (group + d) % 4) for d in range(1, 4)]
    sibling = (coil, group + 1 - 2 * core)

    def side_of(s):
        first_x, pairing = STREAMS[s]
        i = x if first_x else y
        return ((i + 1) // 2) % 2 if pairing == 1 else i // 2

    def part_of(s, k, mine):
        return k * 8 + s * 2 + (side_of(s) if mine else 1 - side_of(s))

    loads = [
        pltpu.make_async_copy(plane_hbm, plane, load_sem.at[0]),
        pltpu.make_async_copy(sens_hbm, sens_v, load_sem.at[1]),
    ]
    kloads = [
        pltpu.make_async_copy(
            kdata_hbm.at[:, pl.ds(q * (parts // 4), parts // 4)],
            kd.at[:, pl.ds(q * (parts // 4), parts // 4)],
            load_sem.at[2 + q],
        )
        for q in range(4)
    ]
    iloads = [
        pltpu.make_async_copy(
            interp_hbm.at[pl.ds(q * (angles // 4), angles // 4)],
            itp.at[pl.ds(q * (angles // 4), angles // 4)],
            load_sem.at[6 + q],
        )
        for q in range(4)
    ]
    for copy in loads + kloads + iloads:
        copy.start()

    barrier = pltpu.get_barrier_semaphore()
    peers = [dev(*stream, over_z) for stream in STREAMS for over_z in (False, True)] + [zdev] + kzdevs
    for peer in peers:
        pl.semaphore_signal(barrier, inc=1, device_id=peer, device_id_type=MESH)

    for copy in loads:
        copy.wait()
    row = lax.broadcasted_iota(jnp.int32, (side, side), 0)
    col = lax.broadcasted_iota(jnp.int32, (side, side), 1)
    perm = jnp.where(jnp.bitwise_xor(row, col) == coil * 8, 1.0, 0.0).astype(BF16)
    for r in range(2):
        sensp[r] = jnp.dot(perm, sens_v[r], preferred_element_type=F32)

    pl.semaphore_wait(barrier, len(peers))

    def sens_copy(s):
        return pltpu.make_async_remote_copy(
            src_ref=sensp.at[core], dst_ref=senso.at[s, core],
            send_sem=sens_send.at[0, s], recv_sem=sens_recv.at[0, s],
            device_id=dev(*STREAMS[s]), device_id_type=MESH,
        )

    def sens_pass(s, r):
        return pltpu.make_async_remote_copy(
            src_ref=senso.at[s, r], dst_ref=senso.at[s, r],
            send_sem=sens_send.at[1, s], recv_sem=sens_recv.at[1, s],
            device_id=sibling, device_id_type=MESH,
        )

    for s in range(4):
        sens_copy(s).start()

    cos_p = jnp.dot(perm, plane[0:side, 0:side], preferred_element_type=F32).astype(BF16)
    sin_p = jnp.dot(perm, plane[side : 2 * side, 0:side], preferred_element_type=F32).astype(BF16)
    blocks = jnp.broadcast_to(block_ref[0:1, :], (side, hits))
    yrow = lax.broadcasted_iota(jnp.int32, (side, hits), 0)
    for h in range(2):
        onto = jnp.where(blocks == yrow * 2 + h, 1.0, 0.0).astype(BF16)
        cos_g = jnp.dot(cos_p, onto, preferred_element_type=F32)
        sin_g = jnp.dot(sin_p, onto, preferred_element_type=F32)
        tab[h, 0:side, 0:hits] = cos_g.astype(BF16)
        tab[h, side : 2 * side, hits : 2 * hits] = cos_g.astype(BF16)
        tab[h, 0:side, hits : 2 * hits] = sin_g.astype(BF16)
        tab[h, side : 2 * side, 0:hits] = (-sin_g).astype(BF16)

    arow = lax.broadcasted_iota(jnp.int32, (angles, spokes), 0)
    scol = lax.broadcasted_iota(jnp.int32, (angles, spokes), 1)
    match = jnp.broadcast_to(angle_ref[0:1, :], (angles, spokes)) == arow
    for q in range(4):
        kloads[q].wait()

        def bin_one(i, carry):
            p = q * (parts // 4) + i
            used = jnp.logical_and(match, scol < count_ref[p])
            weights = jnp.where(used, 1.0, 0.0).astype(BF16)
            for r in range(2):
                summed = jnp.dot(weights, kd[r, p], preferred_element_type=F32)
                for g in range(segs):
                    start = g * angles * BPAD + r * parts + p
                    binned[pl.ds(start, angles, stride=BPAD), :] = summed[:, g * seg : (g + 1) * seg]
            return carry

        lax.fori_loop(0, parts // 4, bin_one, 0)

    batch = 4
    for q in range(4):
        iloads[q].wait()

        def spread_some(i, carry):
            for k in range(batch):
                a = q * (angles // 4) + i * batch + k
                for g in range(segs):
                    start = pl.multiple_of(g * angles * BPAD + a * BPAD, 8)
                    piece = binned[pl.ds(start, 2 * parts), :].astype(BF16)
                    got = jnp.dot(piece, itp[a, g], preferred_element_type=F32)
                    spread[pl.ds(a * segs + g, 2 * parts, stride=xpad), :] = got
            return carry

        lax.fori_loop(0, angles // 4 // batch, spread_some, 0)

    def seg_rows(p, r):
        return pl.ds(pl.multiple_of((r * parts + p) * xpad, 8), hits)

    def seg_copy(s, k, r):
        return pltpu.make_async_remote_copy(
            src_ref=spread.at[seg_rows(part_of(s, k, False), r)], dst_ref=other.at[s, k, r],
            send_sem=send_sem.at[0, s], recv_sem=seg_recv.at[s, k, r],
            device_id=dev(*STREAMS[s]), device_id_type=MESH,
        )

    for k in range(2):
        for s in range(4):
            for r in range(2):
                seg_copy(s, k, r).start()
    for s in range(4):
        sens_copy(s).wait_recv()
        sens_pass(s, core).start()
    for s in range(4):
        sens_pass(s, 1 - core).wait_recv()

    def slots(pairing):
        return (1, 0, 1, 3) if pairing == 1 else (2, 1, 0, 1)

    def lay(s):
        first_x, pairing = STREAMS[s]
        return (first_x, 3, 2, 1, 0) if pairing == 1 else (first_x, 1, 1, 0, 1)

    def make(s, k):
        first_x, pairing = STREAMS[s]
        for r in range(2):
            seg_copy(s, k, r).wait_recv()
        p = part_of(s, k, True)
        rows = []
        for r in range(2):
            own = spread[seg_rows(p, r), :].astype(BF16)
            rows.append(jnp.concatenate([own, other[s, k, r].astype(BF16)], axis=1))
        stacked = jnp.concatenate(rows, axis=0)
        for h in range(2):
            got = jnp.dot(tab[h], stacked, preferred_element_type=F32).astype(BF16)
            for n in range(2):
                for r in range(2):
                    half[n, :, r * side + h * seg : r * side + (h + 1) * seg] = got[
                        r * side : (r + 1) * side, n * seg : (n + 1) * seg
                    ]
        mine = jnp.dot(half[0], plane[...], preferred_element_type=F32)
        theirs = jnp.dot(half[1], plane[...], preferred_element_type=F32)
        for jx in range(4):
            for jy in range(4):
                here = slice((jx * 4 + jy) * 16, (jx * 4 + jy + 1) * 16)
                there = (jx ^ pairing) * 4 + jy if first_x else jx * 4 + (jy ^ pairing)
                that = slice(there * 16, (there + 1) * 16)
                a_re, a_im = sensp[0, here, :], sensp[1, here, :]
                b_re, b_im = senso[s, 0, that, :], senso[s, 1, that, :]
                o_re, o_im = mine[here, 0:side], mine[here, side : 2 * side]
                t_re, t_im = theirs[here, 0:side], theirs[here, side : 2 * side]
                img[s, k, 0, jx, jy] = (a_re * o_re + a_im * o_im) + (b_re * t_re + b_im * t_im)
                img[s, k, 1, jx, jy] = (a_re * o_im - a_im * o_re) + (b_re * t_im - b_im * t_re)

    def copies(s, stage, k, r):
        first_x, second, sent2, slot0, slot_t = lay(s)
        pairing = STREAMS[s][1]
        sent, keep, onward, quarter = slots(pairing)
        if stage == 2:
            if first_x:
                return img.at[s, k, r, pl.ds(sent2, 2)], r2x.at[s, k, r], dev(True, second)
            return img.at[s, k, r, :, pl.ds(sent2, 2)], r2y.at[s - 2, k, r], dev(False, second)
        if stage == 3:
            if first_x:
                return r2x.at[s, k, r, :, pl.ds(sent, 2)], r3.at[s, k, r], dev(False, pairing)
            return r2y.at[s - 2, k, r, pl.ds(sent, 2)], r3.at[s, k, r], dev(True, pairing)
        src = r3.at[s, k, r, :, onward] if first_x else r3.at[s, k, r, onward]
        return src, r4.at[s, k, r], dev(not first_x, second)

    def remote(s, stage, k, r):
        src, dst, peer = copies(s, stage, k, r)
        return pltpu.make_async_remote_copy(
            src_ref=src, dst_ref=dst,
            send_sem=send_sem.at[stage - 1, s], recv_sem=recv_sem.at[stage - 2, s, k, r],
            device_id=peer, device_id_type=MESH,
        )

    def held(s, k, r, pair, quarter):
        first_x, second, sent2, slot0, slot_t = lay(s)
        j = STREAMS[s][1] if pair else 0
        slot = slot_t if pair else slot0
        if first_x:
            return img[s, k, r, j, quarter] + r2x[s, k, r, slot, quarter]
        return img[s, k, r, quarter, j] + r2y[s - 2, k, r, quarter, slot]

    def held3(s, k, r, pair, which, quarter):
        first_x, second, sent2, slot0, slot_t = lay(s)
        slot = slot_t if pair else slot0
        got = r3[s, k, r, slot, which] if first_x else r3[s, k, r, which, slot]
        return held(s, k, r, pair, quarter) + got

    def owner_copies(s, k, r):
        first_x, second, sent2, slot0, slot_t = lay(s)
        spots = ((slot_t, 0), (slot0, 8), (slot_t, 8))
        to = (dev(*STREAMS[s]), zdev, dev(*STREAMS[s], True))
        return [
            pltpu.make_async_remote_copy(
                src_ref=r4.at[s, k, r, slot, pl.ds(start, 8)], dst_ref=r5.at[s, k, r, n],
                send_sem=own_send.at[n, s], recv_sem=own_recv.at[n, s, k, r],
                device_id=to[n], device_id_type=MESH,
            )
            for n, (slot, start) in enumerate(spots)
        ]

    def step(stage, k, r):
        for s in range(4):
            first_x, second, sent2, slot0, slot_t = lay(s)
            sent, keep, onward, quarter = slots(STREAMS[s][1])
            if 3 <= stage <= 5:
                remote(s, stage - 1, k, r).wait_recv()
            if stage == 3:
                for pair in (False, True):
                    slot = slot_t if pair else slot0
                    for q in (sent, sent + 1):
                        value = held(s, k, r, pair, q)
                        if first_x:
                            r2x[s, k, r, slot, q] = value
                        else:
                            r2y[s - 2, k, r, q, slot] = value
            elif stage == 4:
                for pair in (False, True):
                    slot = slot_t if pair else slot0
                    value = held3(s, k, r, pair, onward, quarter)
                    if first_x:
                        r3[s, k, r, slot, onward] = value
                    else:
                        r3[s, k, r, onward, slot] = value
            elif stage == 5:
                for pair in (False, True):
                    slot = slot_t if pair else slot0
                    r4[s, k, r, slot] += held3(s, k, r, pair, keep, 0)
                for copy in owner_copies(s, k, r):
                    copy.start()
            elif stage == 6:
                for copy in owner_copies(s, k, r):
                    copy.wait_recv()
                first = r4[s, k, r, slot0, 0:8, :] + r5[s, k, r, 1]
                second_sum = r5[s, k, r, 0] + r5[s, k, r, 2]
                for h in range(2):
                    cols = slice(h * seg, (h + 1) * seg)
                    gath[group, r, h, part_of(s, k, True)] = first[:, cols]
                    gath[group, r, h, part_of(s, k, False)] = second_sum[:, cols]
            if stage < 5:
                remote(s, stage, k, r).start()

    def kz_remote(d, k, r, slot):
        where = gath.at[slot, r, :, pl.ds(k * 8, 8)]
        return pltpu.make_async_remote_copy(
            src_ref=where, dst_ref=where,
            send_sem=kz_send.at[d], recv_sem=kz_recv.at[slot, k, r],
            device_id=kzdevs[d], device_id_type=MESH,
        )

    def images(k, carry):
        for s in range(4):
            make(s, k)
            for r in range(2):
                remote(s, 2, k, r).start()
        return carry

    lax.fori_loop(0, 2, images, 0)

    def pipeline(i, carry):
        for stage in range(3, 7):
            c = i - (stage - 3)

            @pl.when(jnp.logical_and(c >= 0, c < 4))
            def _():
                k, r = c // 2, c % 2
                step(stage, k, r)
                if stage == 6:
                    for d in range(3):
                        kz_remote(d, k, r, group).start()

        return carry

    lax.fori_loop(0, 7, pipeline, 0)

    for c in range(4):
        for d in range(3):
            kz_remote(d, c // 2, c % 2, (group + d + 1) % 4).wait_recv()

    for mh in range(2):
        for yy in range(8):
            pieces = []
            for g in range(4):
                for r in range(2):
                    pieces.append(gath[g, r, mh, :, yy, :])
            stacked = jnp.concatenate(pieces, axis=0)
            got = jnp.dot(ztab_ref[group], stacked, preferred_element_type=F32, precision=lax.Precision.HIGHEST)
            kzout[mh, pl.ds(yy, 2 * parts, stride=8), :] = got
        out_ref[:, :, :, mh * seg : (mh + 1) * seg] = kzout[mh].reshape(2, parts, 8, seg)

    def sent_all(ref, sem, unused, peer):
        pltpu.make_async_remote_copy(
            src_ref=ref, dst_ref=ref, send_sem=sem, recv_sem=unused, device_id=peer, device_id_type=MESH
        ).wait_send()

    both = pl.ds(0, 2)
    for s in range(4):
        sens_copy(s).wait_send()
        sens_pass(s, core).wait_send()
        sent_all(other.at[s], send_sem.at[0, s], seg_recv.at[s, 0, 0], zdev)
        for stage in range(2, 5):
            src, dst, peer = copies(s, stage, both, both)
            sent_all(src, send_sem.at[stage - 1, s], recv_sem.at[stage - 2, s, 0, 0], peer)
        for n in range(3):
            sent_all(r5.at[s, :, :, n], own_send.at[n, s], own_recv.at[n, s, 0, 0], zdev)
    for d in range(3):
        sent_all(gath.at[group], kz_send.at[d], kz_recv.at[group, 0, 0], kzdevs[d])


def per_device(kdata, spoke_angle, spoke_count, block_index, interp, sens_maps):
    side = sens_maps.shape[2]
    parts = kdata.shape[1]
    spokes, samples = kdata.shape[3], kdata.shape[4]
    angles, segs, seg = interp.shape[0], interp.shape[1], interp.shape[2]
    hits = angles * segs
    any_spec = pl.BlockSpec(memory_space=pl.ANY)
    vmem_spec = pl.BlockSpec(memory_space=pltpu.VMEM)
    return pl.pallas_call(
        functools.partial(kernel, parts, angles, spokes, side),
        out_shape=jax.ShapeDtypeStruct((2, parts, 8, side), F32),
        in_specs=[pl.BlockSpec(memory_space=pltpu.SMEM)] + [vmem_spec] * 3 + [any_spec] * 4,
        out_specs=vmem_spec,
        scratch_shapes=[
            pltpu.VMEM((2, parts, spokes, samples), BF16),
            pltpu.VMEM((angles, segs, seg, seg), BF16),
            pltpu.VMEM((2, side, side), BF16),
            pltpu.VMEM((2 * side, 2 * side), BF16),
            pltpu.VMEM((2, 2 * side, 2 * hits), BF16),
            pltpu.VMEM((2, side, side), F32),
            pltpu.VMEM((4, 2, side, side), F32),
            pltpu.VMEM((segs * angles * BPAD, seg), F32),
            pltpu.VMEM((2 * parts * (hits + 8), seg), F32),
            pltpu.VMEM((4, 2, 2, hits, seg), F32),
            pltpu.VMEM((2, side, 2 * side), BF16),
            pltpu.VMEM((4, 2, 2, 4, 4, 16, side), F32),
            pltpu.VMEM((2, 2, 2, 2, 4, 16, side), F32),
            pltpu.VMEM((2, 2, 2, 4, 2, 16, side), F32),
            pltpu.VMEM((4, 2, 2, 2, 2, 16, side), F32),
            pltpu.VMEM((4, 2, 2, 2, 16, side), F32),
            pltpu.VMEM((4, 2, 2, 3, 8, side), F32),
            pltpu.VMEM((4, 2, 2, parts, 8, seg), F32),
            pltpu.VMEM((2, 2 * parts * 8, seg), F32),
            pltpu.SemaphoreType.DMA((10,)),
            pltpu.SemaphoreType.DMA((2, 4)),
            pltpu.SemaphoreType.DMA((2, 4)),
            pltpu.SemaphoreType.DMA((4, 4)),
            pltpu.SemaphoreType.DMA((4, 2, 2)),
            pltpu.SemaphoreType.DMA((3, 4, 2, 2)),
            pltpu.SemaphoreType.DMA((3, 4)),
            pltpu.SemaphoreType.DMA((3, 4, 2, 2)),
            pltpu.SemaphoreType.DMA((3,)),
            pltpu.SemaphoreType.DMA((4, 2, 2)),
        ],
        compiler_params=pltpu.CompilerParams(
            collective_id=0, has_side_effects=True, vmem_limit_bytes=63 << 20
        ),
    )(
        spoke_count,
        spoke_angle.reshape(1, spokes),
        block_index.reshape(1, hits),
        kz_table(4, parts),
        kdata[:, :, 0],
        interp,
        sens_maps[:, 0],
        plane_table(side),
    )


def solution(mesh):
    placed = (
        P(None, "kz", "coil", None, None),
        P(),
        P("kz"),
        P(),
        P(),
        P(None, "coil", None, None),
    )
    return jax.shard_map(
        per_device,
        mesh=mesh,
        in_specs=placed,
        out_specs=P(None, "kz", "coil", None),
        check_vma=False,
    )
```

time: 81.1 us -> 73.5 us (0.906)
  Pallas kernels: 77.8 us -> 70.1 us
    pallas_call x1, Pallas kernels: 77.8 us -> 70.1 us  [per_device(): pl.pallas_call(functools.partial(kernel, parts, angles, spokes, side), ou...]
where the time goes in v3:
time: 73.5 us; the launch traced here: 73.3 us
  Pallas kernels  70.1 us (95%)
  local copies, waits for them, and re-layouts  3.11 us (4%)
    pallas_call x1, Pallas kernels, per_device(): pl.pallas_call(functools.partial(kernel, parts, angles, spokes, side), ou...  70.1 us
    unnamed x2, local copies, waits for them, and re-layouts  2.44 us

profile of v3, /device:TPU:1, one launch (start us, length us, event | category | flops | bytes accessed | tf_op | source)
XLA Modules:
  0.0 73.3 jit_solution(2987036872716322041)
XLA Ops:
  0.0 0.8 %copy.10 = s32[64,4]{1,0:T(8,128)S(1)} copy(s32[64,4]{0,1:T(4,128)} %param.11) | data formatting | bytes 2048 | tf_op args[3]
  0.8 0.7 reshape.7.block_ref
  1.4 70.1 %shard_map.82 = f32[2,16,8,256]{3,2,1,0:T(8,128)} custom-call(s32[16]{0:T(128)} %count_ref.1, s32[1,256]{1,0:T(1,128)} %bitcast.5, s32[1,256]{1,0:T(1,128)} %reshape.7.block_ref, f32[4,32,128]{2,1,0:T(8,128)} %constant.4.clone.ztab_ref, bf16[2,16,256,512]{3,2,1,0:T(8,128)(2,1)} %bitcast.3, bf16[64,4,128,128]{3,2,1,0:T(8,128)(2,1)} %interp_hbm.1, ...), custom_call_target="tpu_custom_call" | custom-call | tf_op jit(solution)/shard_map/pallas_call | solution.py:414
  71.6 1.7 %copy.12 = f32[2,16,8,256]{3,2,1,0:T(8,128)} copy(f32[2,16,8,256]{3,2,1,0:T(8,128)} %shard_map.82) | data formatting | bytes 524288

commit v4 on v3

--- a/solution.py
+++ b/solution.py
@@ -73,8 +73,9 @@
         return ((x * 4 + flip(y, pairing)) * 2 + zz, group)
 
     zdev = ((x * 4 + y) * 2 + 1 - z, group)
-    kzdevs = [(coil, (group + d) % 4) for d in range(1, 4)]
-    sibling = (coil, group + 1 - 2 * core)
+    beside = group + 1 - 2 * core
+    sibling = (coil, beside)
+    across = (coil, (group + 2) % 4)
 
     def side_of(s):
         first_x, pairing = STREAMS[s]
@@ -88,27 +89,20 @@
         pltpu.make_async_copy(plane_hbm, plane, load_sem.at[0]),
         pltpu.make_async_copy(sens_hbm, sens_v, load_sem.at[1]),
     ]
-    kloads = [
-        pltpu.make_async_copy(
-            kdata_hbm.at[:, pl.ds(q * (parts // 4), parts // 4)],
-            kd.at[:, pl.ds(q * (parts // 4), parts // 4)],
-            load_sem.at[2 + q],
-        )
-        for q in range(4)
-    ]
-    iloads = [
-        pltpu.make_async_copy(
-            interp_hbm.at[pl.ds(q * (angles // 4), angles // 4)],
-            itp.at[pl.ds(q * (angles // 4), angles // 4)],
-            load_sem.at[6 + q],
-        )
-        for q in range(4)
-    ]
-    for copy in loads + kloads + iloads:
+
+    def kload(q):
+        rows = pl.ds(q * (parts // 4), parts // 4)
+        return pltpu.make_async_copy(kdata_hbm.at[:, rows], kd.at[:, rows], load_sem.at[2 + q])
+
+    def iload(q):
+        rows = pl.ds(q * (angles // 4), angles // 4)
+        return pltpu.make_async_copy(interp_hbm.at[rows], itp.at[rows], load_sem.at[6 + q])
+
+    for copy in loads + [kload(q) for q in range(4)] + [iload(q) for q in range(4)]:
         copy.start()
 
     barrier = pltpu.get_barrier_semaphore()
-    peers = [dev(*stream, over_z) for stream in STREAMS for over_z in (False, True)] + [zdev] + kzdevs
+    peers = [dev(*stream, over_z) for stream in STREAMS for over_z in (False, True)] + [zdev, sibling, across]
     for peer in peers:
         pl.semaphore_signal(barrier, inc=1, device_id=peer, device_id_type=MESH)
 
@@ -120,8 +114,6 @@
     for r in range(2):
         sensp[r] = jnp.dot(perm, sens_v[r], preferred_element_type=F32)
 
-    pl.semaphore_wait(barrier, len(peers))
-
     def sens_copy(s):
         return pltpu.make_async_remote_copy(
             src_ref=sensp.at[core], dst_ref=senso.at[s, core],
@@ -136,12 +128,10 @@
             device_id=sibling, device_id_type=MESH,
         )
 
-    for s in range(4):
-        sens_copy(s).start()
-
     cos_p = jnp.dot(perm, plane[0:side, 0:side], preferred_element_type=F32).astype(BF16)
     sin_p = jnp.dot(perm, plane[side : 2 * side, 0:side], preferred_element_type=F32).astype(BF16)
-    blocks = jnp.broadcast_to(block_ref[0:1, :], (side, hits))
+    blocks = jnp.concatenate([block_ref[g : g + 1, :] for g in range(segs)], axis=1)
+    blocks = jnp.broadcast_to(blocks, (side, hits))
     yrow = lax.broadcasted_iota(jnp.int32, (side, hits), 0)
     for h in range(2):
         onto = jnp.where(blocks == yrow * 2 + h, 1.0, 0.0).astype(BF16)
@@ -155,10 +145,9 @@
     arow = lax.broadcasted_iota(jnp.int32, (angles, spokes), 0)
     scol = lax.broadcasted_iota(jnp.int32, (angles, spokes), 1)
     match = jnp.broadcast_to(angle_ref[0:1, :], (angles, spokes)) == arow
-    for q in range(4):
-        kloads[q].wait()
-
-        def bin_one(i, carry):
+    def bin_some(q, carry):
+        kload(q).wait()
+        for i in range(parts // 4):
             p = q * (parts // 4) + i
             used = jnp.logical_and(match, scol < count_ref[p])
             weights = jnp.where(used, 1.0, 0.0).astype(BF16)
@@ -167,25 +156,27 @@
                 for g in range(segs):
                     start = g * angles * BPAD + r * parts + p
                     binned[pl.ds(start, angles, stride=BPAD), :] = summed[:, g * seg : (g + 1) * seg]
-            return carry
-
-        lax.fori_loop(0, parts // 4, bin_one, 0)
-
-    batch = 4
-    for q in range(4):
-        iloads[q].wait()
-
-        def spread_some(i, carry):
-            for k in range(batch):
-                a = q * (angles // 4) + i * batch + k
-                for g in range(segs):
-                    start = pl.multiple_of(g * angles * BPAD + a * BPAD, 8)
-                    piece = binned[pl.ds(start, 2 * parts), :].astype(BF16)
-                    got = jnp.dot(piece, itp[a, g], preferred_element_type=F32)
-                    spread[pl.ds(a * segs + g, 2 * parts, stride=xpad), :] = got
-            return carry
-
-        lax.fori_loop(0, angles // 4 // batch, spread_some, 0)
+        return carry
+
+    lax.fori_loop(0, 4, bin_some, 0)
+
+    pl.semaphore_wait(barrier, len(peers))
+
+    for s in range(4):
+        sens_copy(s).start()
+
+    def spread_some(q, carry):
+        iload(q).wait()
+        for k in range(angles // 4):
+            a = q * (angles // 4) + k
+            for g in range(segs):
+                start = pl.multiple_of(g * angles * BPAD + a * BPAD, 8)
+                piece = binned[pl.ds(start, 2 * parts), :].astype(BF16)
+                got = jnp.dot(piece, itp[a, g], preferred_element_type=F32)
+                spread[pl.ds(g * angles + a, 2 * parts, stride=xpad), :] = got
+        return carry
+
+    lax.fori_loop(0, 4, spread_some, 0)
 
     def seg_rows(p, r):
         return pl.ds(pl.multiple_of((r * parts + p) * xpad, 8), hits)
@@ -336,12 +327,12 @@
             if stage < 5:
                 remote(s, stage, k, r).start()
 
-    def kz_remote(d, k, r, slot):
+    def kz_remote(n, k, r, slot, peer):
         where = gath.at[slot, r, :, pl.ds(k * 8, 8)]
         return pltpu.make_async_remote_copy(
             src_ref=where, dst_ref=where,
-            send_sem=kz_send.at[d], recv_sem=kz_recv.at[slot, k, r],
-            device_id=kzdevs[d], device_id_type=MESH,
+            send_sem=kz_send.at[n], recv_sem=kz_recv.at[slot, k, r],
+            device_id=peer, device_id_type=MESH,
         )
 
     def images(k, carry):
@@ -353,25 +344,27 @@
 
     lax.fori_loop(0, 2, images, 0)
 
-    def pipeline(i, carry):
-        for stage in range(3, 7):
-            c = i - (stage - 3)
-
-            @pl.when(jnp.logical_and(c >= 0, c < 4))
-            def _():
-                k, r = c // 2, c % 2
-                step(stage, k, r)
-                if stage == 6:
-                    for d in range(3):
-                        kz_remote(d, k, r, group).start()
-
-        return carry
-
-    lax.fori_loop(0, 7, pipeline, 0)
-
+    for stage in range(3, 7):
+
+        def stage_items(c, carry):
+            k, r = c // 2, c % 2
+            step(stage, k, r)
+            if stage == 6:
+                kz_remote(0, k, r, group, across).start()
+                kz_remote(1, k, r, group, sibling).start()
+            return carry
+
+        lax.fori_loop(0, 4, stage_items, 0)
+
+    far = (group + 2) % 4
     for c in range(4):
-        for d in range(3):
-            kz_remote(d, c // 2, c % 2, (group + d + 1) % 4).wait_recv()
+        k, r = c // 2, c % 2
+        kz_remote(0, k, r, far, across).wait_recv()
+        kz_remote(2, k, r, far, sibling).start()
+    for c in range(4):
+        k, r = c // 2, c % 2
+        kz_remote(1, k, r, beside, sibling).wait_recv()
+        kz_remote(2, k, r, (beside + 2) % 4, sibling).wait_recv()
 
     for mh in range(2):
         for yy in range(8):
@@ -399,8 +392,8 @@
             sent_all(src, send_sem.at[stage - 1, s], recv_sem.at[stage - 2, s, 0, 0], peer)
         for n in range(3):
             sent_all(r5.at[s, :, :, n], own_send.at[n, s], own_recv.at[n, s, 0, 0], zdev)
-    for d in range(3):
-        sent_all(gath.at[group], kz_send.at[d], kz_recv.at[group, 0, 0], kzdevs[d])
+    for n in range(3):
+        sent_all(gath.at[group], kz_send.at[n], kz_recv.at[group, 0, 0], sibling)
 
 
 def per_device(kdata, spoke_angle, spoke_count, block_index, interp, sens_maps):
@@ -453,7 +446,7 @@
     )(
         spoke_count,
         spoke_angle.reshape(1, spokes),
-        block_index.reshape(1, hits),
+        block_index.T,
         kz_table(4, parts),
         kdata[:, :, 0],
         interp,

time: 73.5 us -> 66.8 us (0.909)
  Pallas kernels: 70.1 us -> 64.9 us
  local copies, waits for them, and re-layouts: 3.11 us -> 1.67 us
    pallas_call x1, Pallas kernels: 70.1 us -> 64.9 us  [per_device(): pl.pallas_call(functools.partial(kernel, parts, angles, spokes, side), ou...]
    unnamed x2 -> x1, local copies, waits for them, and re-layouts: 2.44 us -> 1.67 us
where the time goes in v4:
time: 66.8 us; the launch traced here: 66.6 us
  Pallas kernels  64.9 us (97%)
  local copies, waits for them, and re-layouts  1.67 us (2%)
    pallas_call x1, Pallas kernels, per_device(): pl.pallas_call(functools.partial(kernel, parts, angles, spokes, side), ou...  64.9 us
    unnamed x1, local copies, waits for them, and re-layouts  1.67 us

profile of v4, /device:TPU:1, one launch (start us, length us, event | category | flops | bytes accessed | tf_op | source)
XLA Modules:
  0.0 66.6 jit_solution(12047695179538149453)
XLA Ops:
  0.0 64.9 %shard_map.82 = f32[2,16,8,256]{3,2,1,0:T(8,128)} custom-call(s32[16]{0:T(128)} %count_ref.1, s32[1,256]{1,0:T(1,128)} %bitcast.7, s32[4,64]{1,0:T(4,128)} %bitcast.6, f32[4,32,128]{2,1,0:T(8,128)} %constant.4.clone.ztab_ref, bf16[2,16,256,512]{3,2,1,0:T(8,128)(2,1)} %bitcast.4, bf16[64,4,128,128]{3,2,1,0:T(8,128)(2,1)} %interp_hbm.1, ...), custom_call_target="tpu_custom_call" | custom-call | tf_op jit(solution)/shard_map/pallas_call | solution.py:407
  64.9 1.7 %copy.10 = f32[2,16,8,256]{3,2,1,0:T(8,128)} copy(f32[2,16,8,256]{3,2,1,0:T(8,128)} %shard_map.82) | data formatting | bytes 524288

commit v5 on v4

--- a/solution.py
+++ b/solution.py
@@ -12,6 +12,10 @@
 BF16 = jnp.bfloat16
 MESH = pl.DeviceIdType.MESH
 
+EARLY = ((0, 1, 2, 3), (4, 5, 6, 7))
+BETWEEN = (((), (), (), ()), ((), (), (), ()))
+PLAN = [(w, c) for w in "34" for c in range(8)] + [(w, c) for w in "XF" for c in range(4)]
+BARRIER_AT = 1
 BPAD = 40
 
 STREAMS = ((True, 1), (True, 3), (False, 1), (False, 3))
@@ -50,11 +54,11 @@
 
 def kernel(
     parts, angles, spokes, side,
-    count_ref, angle_ref, block_ref, ztab_ref,
+    count_ref, angle_ref, block_ref,
     kdata_hbm, interp_hbm, sens_hbm, plane_hbm,
-    out_ref,
+    gath,
     kd, itp, sens_v, plane, tab, sensp, senso, binned, spread, other, half,
-    img, r2x, r2y, r3, r4, r5, gath, kzout,
+    img, r2x, r2y, r3, r4, xbuf, rx,
     load_sem, sens_send, sens_recv, send_sem, seg_recv, recv_sem, own_send, own_recv, kz_send, kz_recv,
 ):
     segs = 4
@@ -66,16 +70,19 @@
     core = group % 2
     x, y, z = coil // 8, (coil // 2) % 4, coil % 2
 
-    def dev(axis_x, pairing, over_z=False):
+    beside = group + 1 - 2 * core
+    far = (group + 2) % 4
+    sibling = (coil, beside)
+
+    def dev(axis_x, pairing, over_z=0, over_kz=0):
         zz = 1 - z if over_z else z
+        there = far if over_kz else group
         if axis_x:
-            return ((flip(x, pairing) * 4 + y) * 2 + zz, group)
-        return ((x * 4 + flip(y, pairing)) * 2 + zz, group)
-
-    zdev = ((x * 4 + y) * 2 + 1 - z, group)
-    beside = group + 1 - 2 * core
-    sibling = (coil, beside)
-    across = (coil, (group + 2) % 4)
+            return ((flip(x, pairing) * 4 + y) * 2 + zz, there)
+        return ((x * 4 + flip(y, pairing)) * 2 + zz, there)
+
+    def zdev(over_z, over_kz):
+        return ((x * 4 + y) * 2 + (1 - z if over_z else z), far if over_kz else group)
 
     def side_of(s):
         first_x, pairing = STREAMS[s]
@@ -102,7 +109,9 @@
         copy.start()
 
     barrier = pltpu.get_barrier_semaphore()
-    peers = [dev(*stream, over_z) for stream in STREAMS for over_z in (False, True)] + [zdev, sibling, across]
+    turns = [(0, 0), (0, 1), (1, 0), (1, 1)]
+    peers = [dev(*stream, *turn) for stream in STREAMS for turn in turns]
+    peers += [zdev(*turn) for turn in turns[1:]] + [sibling]
     for peer in peers:
         pl.semaphore_signal(barrier, inc=1, device_id=peer, device_id_type=MESH)
 
@@ -158,12 +167,11 @@
                     binned[pl.ds(start, angles, stride=BPAD), :] = summed[:, g * seg : (g + 1) * seg]
         return carry
 
-    lax.fori_loop(0, 4, bin_some, 0)
-
+    lax.fori_loop(0, BARRIER_AT, bin_some, 0)
     pl.semaphore_wait(barrier, len(peers))
-
     for s in range(4):
         sens_copy(s).start()
+    lax.fori_loop(BARRIER_AT, 4, bin_some, 0)
 
     def spread_some(q, carry):
         iload(q).wait()
@@ -233,139 +241,183 @@
                 b_re, b_im = senso[s, 0, that, :], senso[s, 1, that, :]
                 o_re, o_im = mine[here, 0:side], mine[here, side : 2 * side]
                 t_re, t_im = theirs[here, 0:side], theirs[here, side : 2 * side]
-                img[s, k, 0, jx, jy] = (a_re * o_re + a_im * o_im) + (b_re * t_re + b_im * t_im)
-                img[s, k, 1, jx, jy] = (a_re * o_im - a_im * o_re) + (b_re * t_im - b_im * t_re)
-
-    def copies(s, stage, k, r):
+                parts_of = (
+                    (a_re * o_re + a_im * o_im) + (b_re * t_re + b_im * t_im),
+                    (a_re * o_im - a_im * o_re) + (b_re * t_im - b_im * t_re),
+                )
+                for r in range(2):
+                    for h in range(2):
+                        img[s, k * 4 + r * 2 + h, jx, jy] = parts_of[r][:, h * seg : (h + 1) * seg]
+
+    def copies(s, stage, c):
         first_x, second, sent2, slot0, slot_t = lay(s)
         pairing = STREAMS[s][1]
         sent, keep, onward, quarter = slots(pairing)
         if stage == 2:
             if first_x:
-                return img.at[s, k, r, pl.ds(sent2, 2)], r2x.at[s, k, r], dev(True, second)
-            return img.at[s, k, r, :, pl.ds(sent2, 2)], r2y.at[s - 2, k, r], dev(False, second)
+                return img.at[s, c, pl.ds(sent2, 2)], r2x.at[s, c], dev(True, second)
+            return img.at[s, c, :, pl.ds(sent2, 2)], r2y.at[s - 2, c], dev(False, second)
         if stage == 3:
             if first_x:
-                return r2x.at[s, k, r, :, pl.ds(sent, 2)], r3.at[s, k, r], dev(False, pairing)
-            return r2y.at[s - 2, k, r, pl.ds(sent, 2)], r3.at[s, k, r], dev(True, pairing)
-        src = r3.at[s, k, r, :, onward] if first_x else r3.at[s, k, r, onward]
-        return src, r4.at[s, k, r], dev(not first_x, second)
-
-    def remote(s, stage, k, r):
-        src, dst, peer = copies(s, stage, k, r)
+                return r2x.at[s, c, :, pl.ds(sent, 2)], r3.at[s, c], dev(False, pairing)
+            return r2y.at[s - 2, c, pl.ds(sent, 2)], r3.at[s, c], dev(True, pairing)
+        src = r3.at[s, c, :, onward] if first_x else r3.at[s, c, onward]
+        return src, r4.at[s, c], dev(not first_x, second)
+
+    def remote(s, stage, c):
+        src, dst, peer = copies(s, stage, c)
         return pltpu.make_async_remote_copy(
             src_ref=src, dst_ref=dst,
-            send_sem=send_sem.at[stage - 1, s], recv_sem=recv_sem.at[stage - 2, s, k, r],
+            send_sem=send_sem.at[stage - 1, s], recv_sem=recv_sem.at[stage - 2, s, c],
             device_id=peer, device_id_type=MESH,
         )
 
-    def held(s, k, r, pair, quarter):
+    def held(s, c, pair, quarter):
         first_x, second, sent2, slot0, slot_t = lay(s)
         j = STREAMS[s][1] if pair else 0
         slot = slot_t if pair else slot0
         if first_x:
-            return img[s, k, r, j, quarter] + r2x[s, k, r, slot, quarter]
-        return img[s, k, r, quarter, j] + r2y[s - 2, k, r, quarter, slot]
-
-    def held3(s, k, r, pair, which, quarter):
+            return img[s, c, j, quarter] + r2x[s, c, slot, quarter]
+        return img[s, c, quarter, j] + r2y[s - 2, c, quarter, slot]
+
+    def held3(s, c, pair, which, quarter):
         first_x, second, sent2, slot0, slot_t = lay(s)
         slot = slot_t if pair else slot0
-        got = r3[s, k, r, slot, which] if first_x else r3[s, k, r, which, slot]
-        return held(s, k, r, pair, quarter) + got
-
-    def owner_copies(s, k, r):
-        first_x, second, sent2, slot0, slot_t = lay(s)
-        spots = ((slot_t, 0), (slot0, 8), (slot_t, 8))
-        to = (dev(*STREAMS[s]), zdev, dev(*STREAMS[s], True))
-        return [
-            pltpu.make_async_remote_copy(
-                src_ref=r4.at[s, k, r, slot, pl.ds(start, 8)], dst_ref=r5.at[s, k, r, n],
-                send_sem=own_send.at[n, s], recv_sem=own_recv.at[n, s, k, r],
-                device_id=to[n], device_id_type=MESH,
-            )
-            for n, (slot, start) in enumerate(spots)
-        ]
-
-    def step(stage, k, r):
+        got = r3[s, c, slot, which] if first_x else r3[s, c, which, slot]
+        return held(s, c, pair, quarter) + got
+
+    def step(stage, c):
         for s in range(4):
             first_x, second, sent2, slot0, slot_t = lay(s)
             sent, keep, onward, quarter = slots(STREAMS[s][1])
-            if 3 <= stage <= 5:
-                remote(s, stage - 1, k, r).wait_recv()
-            if stage == 3:
-                for pair in (False, True):
+            remote(s, stage - 1, c).wait_recv()
+            for pair in range(2):
+                slot = slot_t if pair else slot0
+                if stage == 3:
+                    for q in (sent, sent + 1):
+                        value = held(s, c, pair, q)
+                        if first_x:
+                            r2x[s, c, slot, q] = value
+                        else:
+                            r2y[s - 2, c, q, slot] = value
+                else:
+                    value = held3(s, c, pair, onward, quarter)
+                    if first_x:
+                        r3[s, c, slot, onward] = value
+                    else:
+                        r3[s, c, onward, slot] = value
+            remote(s, stage, c).start()
+
+    def last_copies(kr, pair, s):
+        got = []
+        for jz, jk in turns:
+            n = pair * 4 + jz * 2 + jk
+            if n == 0:
+                continue
+            if pair:
+                src, dst, peer = xbuf.at[1, kr, jz, s], rx.at[n, kr, s], dev(*STREAMS[s], jz, jk)
+            else:
+                src, dst, peer = xbuf.at[0, kr, jz], rx.at[n, kr], zdev(jz, jk)
+            got.append(
+                pltpu.make_async_remote_copy(
+                    src_ref=src, dst_ref=dst, send_sem=own_send.at[n], recv_sem=own_recv.at[n, kr],
+                    device_id=peer, device_id_type=MESH,
+                )
+            )
+        return got
+
+    def last(kr):
+        for s in range(4):
+            first_x, second, sent2, slot0, slot_t = lay(s)
+            keep = slots(STREAMS[s][1])[1]
+            for h in range(2):
+                c = kr * 2 + h
+                remote(s, 4, c).wait_recv()
+                for pair in range(2):
                     slot = slot_t if pair else slot0
-                    for q in (sent, sent + 1):
-                        value = held(s, k, r, pair, q)
-                        if first_x:
-                            r2x[s, k, r, slot, q] = value
-                        else:
-                            r2y[s - 2, k, r, q, slot] = value
-            elif stage == 4:
-                for pair in (False, True):
-                    slot = slot_t if pair else slot0
-                    value = held3(s, k, r, pair, onward, quarter)
-                    if first_x:
-                        r3[s, k, r, slot, onward] = value
-                    else:
-                        r3[s, k, r, onward, slot] = value
-            elif stage == 5:
-                for pair in (False, True):
-                    slot = slot_t if pair else slot0
-                    r4[s, k, r, slot] += held3(s, k, r, pair, keep, 0)
-                for copy in owner_copies(s, k, r):
-                    copy.start()
-            elif stage == 6:
-                for copy in owner_copies(s, k, r):
-                    copy.wait_recv()
-                first = r4[s, k, r, slot0, 0:8, :] + r5[s, k, r, 1]
-                second_sum = r5[s, k, r, 0] + r5[s, k, r, 2]
-                for h in range(2):
-                    cols = slice(h * seg, (h + 1) * seg)
-                    gath[group, r, h, part_of(s, k, True)] = first[:, cols]
-                    gath[group, r, h, part_of(s, k, False)] = second_sum[:, cols]
-            if stage < 5:
-                remote(s, stage, k, r).start()
-
-    def kz_remote(n, k, r, slot, peer):
-        where = gath.at[slot, r, :, pl.ds(k * 8, 8)]
+                    value = r4[s, c, slot] + held3(s, c, pair, keep, 0)
+                    for jz in range(2):
+                        xbuf[pair, kr, jz, s, h] = value[jz * 8 : (jz + 1) * 8]
+            for copy in last_copies(kr, 1, s):
+                copy.start()
+        for copy in last_copies(kr, 0, 0):
+            copy.start()
+
+    def arrived(n, kr):
+        whole = rx.at[n, kr]
+        return pltpu.make_async_remote_copy(
+            src_ref=whole, dst_ref=whole, send_sem=own_send.at[n], recv_sem=own_recv.at[n, kr],
+            device_id=sibling, device_id_type=MESH,
+        )
+
+    def kz_remote(n, kr):
+        slot = far if n else group
+        where = gath.at[slot, kr % 2, :, pl.ds(kr // 2 * 8, 8)]
         return pltpu.make_async_remote_copy(
             src_ref=where, dst_ref=where,
-            send_sem=kz_send.at[n], recv_sem=kz_recv.at[slot, k, r],
-            device_id=peer, device_id_type=MESH,
+            send_sem=kz_send.at[n], recv_sem=kz_recv.at[n, kr],
+            device_id=sibling, device_id_type=MESH,
         )
 
-    def images(k, carry):
+    def finish(kr):
+        k, r = kr // 2, kr % 2
+        for n in range(1, 8):
+            arrived(n, kr).wait_recv()
+        for s in range(4):
+            for h in range(2):
+                gath[group, r, h, part_of(s, k, True)] = xbuf[0, kr, 0, s, h] + rx[2, kr, s, h]
+                gath[group, r, h, part_of(s, k, False)] = rx[4, kr, s, h] + rx[6, kr, s, h]
+                gath[far, r, h, part_of(s, k, True)] = rx[1, kr, s, h] + rx[3, kr, s, h]
+                gath[far, r, h, part_of(s, k, False)] = rx[5, kr, s, h] + rx[7, kr, s, h]
+        for n in range(2):
+            kz_remote(n, kr).start()
+
+    def run(plan):
+        for what, c in plan:
+            if what == "2":
+                for s in range(4):
+                    remote(s, 2, c).start()
+            elif what == "X":
+                last(c)
+            elif what == "F":
+                finish(c)
+            else:
+                step(int(what), c)
+
+    for k in range(2):
         for s in range(4):
             make(s, k)
-            for r in range(2):
-                remote(s, 2, k, r).start()
-        return carry
-
-    lax.fori_loop(0, 2, images, 0)
-
-    for stage in range(3, 7):
-
-        def stage_items(c, carry):
-            k, r = c // 2, c % 2
-            step(stage, k, r)
-            if stage == 6:
-                kz_remote(0, k, r, group, across).start()
-                kz_remote(1, k, r, group, sibling).start()
-            return carry
-
-        lax.fori_loop(0, 4, stage_items, 0)
-
-    far = (group + 2) % 4
-    for c in range(4):
-        k, r = c // 2, c % 2
-        kz_remote(0, k, r, far, across).wait_recv()
-        kz_remote(2, k, r, far, sibling).start()
-    for c in range(4):
-        k, r = c // 2, c % 2
-        kz_remote(1, k, r, beside, sibling).wait_recv()
-        kz_remote(2, k, r, (beside + 2) % 4, sibling).wait_recv()
-
+            for c in EARLY[k]:
+                remote(s, 2, c).start()
+            run(BETWEEN[k][s])
+    run(PLAN)
+
+    for kr in range(4):
+        for n in range(2):
+            kz_remote(n, kr).wait_recv()
+
+    def sent_all(ref, sem, unused, peer):
+        pltpu.make_async_remote_copy(
+            src_ref=ref, dst_ref=ref, send_sem=sem, recv_sem=unused, device_id=peer, device_id_type=MESH
+        ).wait_send()
+
+    everything = pl.ds(0, 8)
+    for s in range(4):
+        sens_copy(s).wait_send()
+        sens_pass(s, core).wait_send()
+        sent_all(other.at[s], send_sem.at[0, s], seg_recv.at[s, 0, 0], sibling)
+        for stage in range(2, 5):
+            src, dst, peer = copies(s, stage, everything)
+            sent_all(src, send_sem.at[stage - 1, s], recv_sem.at[stage - 2, s, 0], peer)
+    for n in range(1, 8):
+        sent_all(rx.at[n], own_send.at[n], own_recv.at[n, 0], sibling)
+    for n in range(2):
+        sent_all(gath.at[group], kz_send.at[n], kz_recv.at[n, 0], sibling)
+
+
+def kz_kernel(parts, ztab_ref, gath, out_ref, kzout):
+    seg = 128
+    group = lax.axis_index("kz")
     for mh in range(2):
         for yy in range(8):
             pieces = []
@@ -377,24 +429,6 @@
             kzout[mh, pl.ds(yy, 2 * parts, stride=8), :] = got
         out_ref[:, :, :, mh * seg : (mh + 1) * seg] = kzout[mh].reshape(2, parts, 8, seg)
 
-    def sent_all(ref, sem, unused, peer):
-        pltpu.make_async_remote_copy(
-            src_ref=ref, dst_ref=ref, send_sem=sem, recv_sem=unused, device_id=peer, device_id_type=MESH
-        ).wait_send()
-
-    both = pl.ds(0, 2)
-    for s in range(4):
-        sens_copy(s).wait_send()
-        sens_pass(s, core).wait_send()
-        sent_all(other.at[s], send_sem.at[0, s], seg_recv.at[s, 0, 0], zdev)
-        for stage in range(2, 5):
-            src, dst, peer = copies(s, stage, both, both)
-            sent_all(src, send_sem.at[stage - 1, s], recv_sem.at[stage - 2, s, 0, 0], peer)
-        for n in range(3):
-            sent_all(r5.at[s, :, :, n], own_send.at[n, s], own_recv.at[n, s, 0, 0], zdev)
-    for n in range(3):
-        sent_all(gath.at[group], kz_send.at[n], kz_recv.at[group, 0, 0], sibling)
-
 
 def per_device(kdata, spoke_angle, spoke_count, block_index, interp, sens_maps):
     side = sens_maps.shape[2]
@@ -404,10 +438,10 @@
     hits = angles * segs
     any_spec = pl.BlockSpec(memory_space=pl.ANY)
     vmem_spec = pl.BlockSpec(memory_space=pltpu.VMEM)
-    return pl.pallas_call(
+    gathered = pl.pallas_call(
         functools.partial(kernel, parts, angles, spokes, side),
-        out_shape=jax.ShapeDtypeStruct((2, parts, 8, side), F32),
-        in_specs=[pl.BlockSpec(memory_space=pltpu.SMEM)] + [vmem_spec] * 3 + [any_spec] * 4,
+        out_shape=jax.ShapeDtypeStruct((4, 2, 2, parts, 8, seg), F32),
+        in_specs=[pl.BlockSpec(memory_space=pltpu.SMEM)] + [vmem_spec] * 2 + [any_spec] * 4,
         out_specs=vmem_spec,
         scratch_shapes=[
             pltpu.VMEM((2, parts, spokes, samples), BF16),
@@ -421,38 +455,43 @@
             pltpu.VMEM((2 * parts * (hits + 8), seg), F32),
             pltpu.VMEM((4, 2, 2, hits, seg), F32),
             pltpu.VMEM((2, side, 2 * side), BF16),
-            pltpu.VMEM((4, 2, 2, 4, 4, 16, side), F32),
-            pltpu.VMEM((2, 2, 2, 2, 4, 16, side), F32),
-            pltpu.VMEM((2, 2, 2, 4, 2, 16, side), F32),
-            pltpu.VMEM((4, 2, 2, 2, 2, 16, side), F32),
-            pltpu.VMEM((4, 2, 2, 2, 16, side), F32),
-            pltpu.VMEM((4, 2, 2, 3, 8, side), F32),
-            pltpu.VMEM((4, 2, 2, parts, 8, seg), F32),
-            pltpu.VMEM((2, 2 * parts * 8, seg), F32),
+            pltpu.VMEM((4, 8, 4, 4, 16, seg), F32),
+            pltpu.VMEM((2, 8, 2, 4, 16, seg), F32),
+            pltpu.VMEM((2, 8, 4, 2, 16, seg), F32),
+            pltpu.VMEM((4, 8, 2, 2, 16, seg), F32),
+            pltpu.VMEM((4, 8, 2, 16, seg), F32),
+            pltpu.VMEM((2, 4, 2, 4, 2, 8, seg), F32),
+            pltpu.VMEM((8, 4, 4, 2, 8, seg), F32),
             pltpu.SemaphoreType.DMA((10,)),
             pltpu.SemaphoreType.DMA((2, 4)),
             pltpu.SemaphoreType.DMA((2, 4)),
             pltpu.SemaphoreType.DMA((4, 4)),
             pltpu.SemaphoreType.DMA((4, 2, 2)),
-            pltpu.SemaphoreType.DMA((3, 4, 2, 2)),
-            pltpu.SemaphoreType.DMA((3, 4)),
-            pltpu.SemaphoreType.DMA((3, 4, 2, 2)),
-            pltpu.SemaphoreType.DMA((3,)),
-            pltpu.SemaphoreType.DMA((4, 2, 2)),
+            pltpu.SemaphoreType.DMA((3, 4, 8)),
+            pltpu.SemaphoreType.DMA((8,)),
+            pltpu.SemaphoreType.DMA((8, 4)),
+            pltpu.SemaphoreType.DMA((2,)),
+            pltpu.SemaphoreType.DMA((2, 4)),
         ],
         compiler_params=pltpu.CompilerParams(
-            collective_id=0, has_side_effects=True, vmem_limit_bytes=63 << 20
+            collective_id=0, has_side_effects=True, vmem_limit_bytes=56 << 20
         ),
     )(
         spoke_count,
         spoke_angle.reshape(1, spokes),
         block_index.T,
-        kz_table(4, parts),
         kdata[:, :, 0],
         interp,
         sens_maps[:, 0],
         plane_table(side),
     )
+    return pl.pallas_call(
+        functools.partial(kz_kernel, parts),
+        out_shape=jax.ShapeDtypeStruct((2, parts, 8, side), F32),
+        in_specs=[vmem_spec, vmem_spec],
+        out_specs=vmem_spec,
+        scratch_shapes=[pltpu.VMEM((2, 2 * parts * 8, seg), F32)],
+    )(kz_table(4, parts), gathered)
 
 
 def solution(mesh):

time: 66.8 us -> 65.3 us (0.978)
  local copies, waits for them, and re-layouts: 1.67 us -> 0 us
    pallas_call x0 -> x1, Pallas kernels: none -> 3.02 us  [per_device(): pl.pallas_call(functools.partial(kz_kernel, parts), out_shape=jax.ShapeDt...]
    pallas_call x1, Pallas kernels: 64.9 us -> 62.1 us  [per_device(): pl.pallas_call(functools.partial(kernel, parts, angles, spokes, side), ou...]
    unnamed x1 -> x0, local copies, waits for them, and re-layouts: 1.67 us -> none
where the time goes in v5:
time: 65.3 us; the launch traced here: 65.2 us
  Pallas kernels  65.2 us (100%)
    pallas_call x1, Pallas kernels, per_device(): pl.pallas_call(functools.partial(kernel, parts, angles, spokes, side), ou...  62.1 us
    pallas_call x1, Pallas kernels, per_device(): pl.pallas_call(functools.partial(kz_kernel, parts), out_shape=jax.ShapeDt...  3.02 us

profile of v5, /device:TPU:1, one launch (start us, length us, event | category | flops | bytes accessed | tf_op | source)
XLA Modules:
  0.0 65.2 jit_solution(5359601810348751467)
XLA Ops:
  0.0 62.1 %shard_map.82.gath = f32[4,2,2,16,8,128]{5,4,3,2,1,0:T(8,128)} custom-call(s32[16]{0:T(128)} %count_ref.1, s32[1,256]{1,0:T(1,128)} %bitcast.7, s32[4,64]{1,0:T(4,128)} %bitcast.6, bf16[2,16,256,512]{3,2,1,0:T(8,128)(2,1)} %bitcast.4, bf16[64,4,128,128]{3,2,1,0:T(8,128)(2,1)} %interp_hbm.1, bf16[2,256,256]{2,1,0:T(8,128)(2,1)} %bitcast.5, ...), custom_call_target="tpu_custom_call" | custom-call | tf_op jit(solution)/shard_map/pallas_call | solution.py:441
  62.1 3.0 %shard_map.83 = f32[2,16,8,256]{3,2,1,0:T(8,128)} custom-call(f32[4,32,128]{2,1,0:T(8,128)} %constant.5.clone.ztab_ref, f32[4,2,2,16,8,128]{5,4,3,2,1,0:T(8,128)} %shard_map.82.gath), custom_call_target="tpu_custom_call" | custom-call | tf_op jit(solution)/shard_map/pallas_call | solution.py:488

commit v6 on v5

--- a/solution.py
+++ b/solution.py
@@ -12,9 +12,7 @@
 BF16 = jnp.bfloat16
 MESH = pl.DeviceIdType.MESH
 
-EARLY = ((0, 1, 2, 3), (4, 5, 6, 7))
-BETWEEN = (((), (), (), ()), ((), (), (), ()))
-PLAN = [(w, c) for w in "34" for c in range(8)] + [(w, c) for w in "XF" for c in range(4)]
+PLAN = (('M', 0, 3), ('M', 0, 2), ('2', 3, 2), ('M', 0, 1), ('2', 3, 1), ('2', 3, 3), ('2', 1, 3), ('2', 2, 3), ('2', 0, 3), ('2', 0, 1), ('M', 0, 0), ('2', 2, 2), ('2', 3, 0), ('2', 0, 2), ('2', 2, 0), ('2', 1, 2), ('2', 0, 0), ('2', 2, 1), ('M', 1, 3), ('M', 1, 1), ('2', 6, 3), ('2', 1, 0), ('2', 1, 1), ('M', 1, 2), ('2', 7, 1), ('2', 7, 2), ('M', 1, 0), ('2', 7, 0), ('2', 4, 1), ('3', 3), ('2', 6, 2), ('3', 2), ('2', 6, 1), ('2', 5, 2), ('2', 7, 3), ('2', 5, 3), ('2', 6, 0), ('3', 1), ('3', 0), ('2', 5, 1), ('2', 4, 3), ('2', 5, 0), ('4', 2), ('4', 3), ('2', 4, 0), ('2', 4, 2), ('3', 7), ('3', 6), ('4', 1), ('4', 0), ('3', 5), ('X', 1), ('3', 4), ('4', 7), ('4', 6), ('X', 0), ('4', 5), ('4', 4), ('X', 3), ('F', 1), ('X', 2), ('F', 0), ('O', 1), ('F', 3), ('O', 0), ('F', 2), ('O', 3), ('O', 2))
 BARRIER_AT = 1
 BPAD = 40
 
@@ -45,7 +43,10 @@
         real = np.concatenate([c, s], axis=2).reshape(parts, -1)
         imag = np.concatenate([-s, c], axis=2).reshape(parts, -1)
         blocks.append(np.concatenate([real, imag], axis=0))
-    return jnp.asarray(np.stack(blocks), dtype=F32)
+    table = np.stack(blocks).astype(np.float32)
+    high = table.astype(jnp.bfloat16)
+    low = (table - high.astype(np.float32)).astype(jnp.bfloat16)
+    return jnp.asarray(np.concatenate([high, low, high], axis=2))
 
 
 def flip(i, pairing):
@@ -56,10 +57,10 @@
     parts, angles, spokes, side,
     count_ref, angle_ref, block_ref,
     kdata_hbm, interp_hbm, sens_hbm, plane_hbm,
-    gath,
+    out_hbm,
     kd, itp, sens_v, plane, tab, sensp, senso, binned, spread, other, half,
-    img, r2x, r2y, r3, r4, xbuf, rx,
-    load_sem, sens_send, sens_recv, send_sem, seg_recv, recv_sem, own_send, own_recv, kz_send, kz_recv,
+    img, r2x, r2y, r3, r4, xbuf, rx, gath,
+    load_sem, sens_send, sens_recv, send_sem, seg_recv, recv_sem, own_send, own_recv, kz_send, kz_recv, out_sem,
 ):
     segs = 4
     seg = 128
@@ -372,29 +373,28 @@
         for n in range(2):
             kz_remote(n, kr).start()
 
-    def run(plan):
-        for what, c in plan:
-            if what == "2":
-                for s in range(4):
-                    remote(s, 2, c).start()
-            elif what == "X":
-                last(c)
-            elif what == "F":
-                finish(c)
-            else:
-                step(int(what), c)
-
-    for k in range(2):
-        for s in range(4):
-            make(s, k)
-            for c in EARLY[k]:
-                remote(s, 2, c).start()
-            run(BETWEEN[k][s])
-    run(PLAN)
-
-    for kr in range(4):
+    def out_copy(kr):
+        rows = (slice(None), kr % 2, slice(None), pl.ds(kr // 2 * 8, 8))
+        return pltpu.make_async_copy(gath.at[rows], out_hbm.at[rows], out_sem.at[kr])
+
+    def put(kr):
         for n in range(2):
             kz_remote(n, kr).wait_recv()
+        out_copy(kr).start()
+
+    for what, *where in PLAN:
+        if what == "M":
+            make(where[1], where[0])
+        elif what == "2":
+            remote(where[1], 2, where[0]).start()
+        elif what == "X":
+            last(*where)
+        elif what == "F":
+            finish(*where)
+        elif what == "O":
+            put(*where)
+        else:
+            step(int(what), *where)
 
     def sent_all(ref, sem, unused, peer):
         pltpu.make_async_remote_copy(
@@ -413,21 +413,22 @@
         sent_all(rx.at[n], own_send.at[n], own_recv.at[n, 0], sibling)
     for n in range(2):
         sent_all(gath.at[group], kz_send.at[n], kz_recv.at[n, 0], sibling)
+    for kr in range(4):
+        out_copy(kr).wait()
 
 
 def kz_kernel(parts, ztab_ref, gath, out_ref, kzout):
-    seg = 128
     group = lax.axis_index("kz")
-    for mh in range(2):
-        for yy in range(8):
-            pieces = []
-            for g in range(4):
-                for r in range(2):
-                    pieces.append(gath[g, r, mh, :, yy, :])
-            stacked = jnp.concatenate(pieces, axis=0)
-            got = jnp.dot(ztab_ref[group], stacked, preferred_element_type=F32, precision=lax.Precision.HIGHEST)
-            kzout[mh, pl.ds(yy, 2 * parts, stride=8), :] = got
-        out_ref[:, :, :, mh * seg : (mh + 1) * seg] = kzout[mh].reshape(2, parts, 8, seg)
+    for yy in range(8):
+        pieces = [gath[g, r, 0, :, yy, :] for g in range(4) for r in range(2)]
+        stacked = jnp.concatenate(pieces, axis=0)
+        high = stacked.astype(BF16)
+        low = (stacked - high.astype(F32)).astype(BF16)
+        got = jnp.dot(
+            ztab_ref[group], jnp.concatenate([high, high, low], axis=0), preferred_element_type=F32
+        )
+        kzout[pl.ds(yy, 2 * parts, stride=8), :] = got
+    out_ref[...] = kzout[...].reshape(2, parts, 8, kzout.shape[1])
 
 
 def per_device(kdata, spoke_angle, spoke_count, block_index, interp, sens_maps):
@@ -442,7 +443,7 @@
         functools.partial(kernel, parts, angles, spokes, side),
         out_shape=jax.ShapeDtypeStruct((4, 2, 2, parts, 8, seg), F32),
         in_specs=[pl.BlockSpec(memory_space=pltpu.SMEM)] + [vmem_spec] * 2 + [any_spec] * 4,
-        out_specs=vmem_spec,
+        out_specs=any_spec,
         scratch_shapes=[
             pltpu.VMEM((2, parts, spokes, samples), BF16),
             pltpu.VMEM((angles, segs, seg, seg), BF16),
@@ -462,6 +463,7 @@
             pltpu.VMEM((4, 8, 2, 16, seg), F32),
             pltpu.VMEM((2, 4, 2, 4, 2, 8, seg), F32),
             pltpu.VMEM((8, 4, 4, 2, 8, seg), F32),
+            pltpu.VMEM((4, 2, 2, parts, 8, seg), F32),
             pltpu.SemaphoreType.DMA((10,)),
             pltpu.SemaphoreType.DMA((2, 4)),
             pltpu.SemaphoreType.DMA((2, 4)),
@@ -472,6 +474,7 @@
             pltpu.SemaphoreType.DMA((8, 4)),
             pltpu.SemaphoreType.DMA((2,)),
             pltpu.SemaphoreType.DMA((2, 4)),
+            pltpu.SemaphoreType.DMA((4,)),
         ],
         compiler_params=pltpu.CompilerParams(
             collective_id=0, has_side_effects=True, vmem_limit_bytes=56 << 20
@@ -487,10 +490,14 @@
     )
     return pl.pallas_call(
         functools.partial(kz_kernel, parts),
+        grid=(2,),
         out_shape=jax.ShapeDtypeStruct((2, parts, 8, side), F32),
-        in_specs=[vmem_spec, vmem_spec],
-        out_specs=vmem_spec,
-        scratch_shapes=[pltpu.VMEM((2, 2 * parts * 8, seg), F32)],
+        in_specs=[
+            pl.BlockSpec((4, 2 * parts, 24 * parts), lambda h: (0, 0, 0)),
+            pl.BlockSpec((4, 2, 1, parts, 8, seg), lambda h: (0, 0, h, 0, 0, 0)),
+        ],
+        out_specs=pl.BlockSpec((2, parts, 8, seg), lambda h: (0, 0, 0, h)),
+        scratch_shapes=[pltpu.VMEM((2 * parts * 8, seg), F32)],
     )(kz_table(4, parts), gathered)
 
 

time: 65.3 us -> 62.8 us (0.962)
  Pallas kernels: 65.2 us -> 62.6 us
    pallas_call x1, Pallas kernels: 62.1 us -> 60 us  [per_device(): pl.pallas_call(functools.partial(kernel, parts, angles, spokes, side), ou...]
where the time goes in v6:
time: 62.8 us; the launch traced here: 62.6 us
  Pallas kernels  62.6 us (100%)
    pallas_call x1, Pallas kernels, per_device(): pl.pallas_call(functools.partial(kernel, parts, angles, spokes, side), ou...  60 us
    pallas_call x1, Pallas kernels, per_device(): pl.pallas_call(functools.partial(kz_kernel, parts), grid=(2,), out_shape=...  2.62 us

profile of v6, /device:TPU:1, one launch (start us, length us, event | category | flops | bytes accessed | tf_op | source)
XLA Modules:
  0.0 62.6 jit_solution(10737018087922104255)
XLA Ops:
  0.0 60.0 %shard_map.82.gath = f32[4,2,2,16,8,128]{5,4,3,2,1,0:T(8,128)} custom-call(s32[16]{0:T(128)} %count_ref.1, s32[1,256]{1,0:T(1,128)} %bitcast.7, s32[4,64]{1,0:T(4,128)} %bitcast.6, bf16[2,16,256,512]{3,2,1,0:T(8,128)(2,1)} %bitcast.4, bf16[64,4,128,128]{3,2,1,0:T(8,128)(2,1)} %interp_hbm.1, bf16[2,256,256]{2,1,0:T(8,128)(2,1)} %bitcast.5, ...), custom_call_target="tpu_custom_call" | custom-call | tf_op jit(solution)/shard_map/pallas_call | solution.py:442
  60.0 2.6 %shard_map.83 = f32[2,16,8,256]{3,2,1,0:T(8,128)} custom-call(bf16[4,32,384]{2,1,0:T(8,128)(2,1)} %constant.5.clone.ztab_ref, f32[4,2,2,16,8,128]{5,4,3,2,1,0:T(8,128)} %shard_map.82.gath), custom_call_target="tpu_custom_call" | custom-call | tf_op jit(solution)/shard_map/pallas_call | solution.py:491

commit v7 on v6

--- a/solution.py
+++ b/solution.py
@@ -12,7 +12,7 @@
 BF16 = jnp.bfloat16
 MESH = pl.DeviceIdType.MESH
 
-PLAN = (('M', 0, 3), ('M', 0, 2), ('2', 3, 2), ('M', 0, 1), ('2', 3, 1), ('2', 3, 3), ('2', 1, 3), ('2', 2, 3), ('2', 0, 3), ('2', 0, 1), ('M', 0, 0), ('2', 2, 2), ('2', 3, 0), ('2', 0, 2), ('2', 2, 0), ('2', 1, 2), ('2', 0, 0), ('2', 2, 1), ('M', 1, 3), ('M', 1, 1), ('2', 6, 3), ('2', 1, 0), ('2', 1, 1), ('M', 1, 2), ('2', 7, 1), ('2', 7, 2), ('M', 1, 0), ('2', 7, 0), ('2', 4, 1), ('3', 3), ('2', 6, 2), ('3', 2), ('2', 6, 1), ('2', 5, 2), ('2', 7, 3), ('2', 5, 3), ('2', 6, 0), ('3', 1), ('3', 0), ('2', 5, 1), ('2', 4, 3), ('2', 5, 0), ('4', 2), ('4', 3), ('2', 4, 0), ('2', 4, 2), ('3', 7), ('3', 6), ('4', 1), ('4', 0), ('3', 5), ('X', 1), ('3', 4), ('4', 7), ('4', 6), ('X', 0), ('4', 5), ('4', 4), ('X', 3), ('F', 1), ('X', 2), ('F', 0), ('O', 1), ('F', 3), ('O', 0), ('F', 2), ('O', 3), ('O', 2))
+PLAN = (('M', 0, 2), ('M', 0, 1), ('M', 0, 3), ('2', 1, 2), ('2', 0, 3), ('2', 0, 1), ('M', 0, 0), ('2', 1, 1), ('2', 3, 0), ('2', 1, 3), ('2', 2, 1), ('2', 0, 2), ('2', 3, 1), ('2', 2, 2), ('2', 2, 3), ('2', 0, 0), ('2', 3, 2), ('2', 1, 0), ('M', 1, 2), ('2', 7, 2), ('M', 1, 3), ('2', 2, 0), ('2', 4, 3), ('M', 1, 1), ('2', 3, 3), ('M', 1, 0), ('2', 5, 0), ('2', 6, 1), ('3', 0), ('2', 5, 2), ('2', 5, 3), ('3', 1), ('2', 4, 1), ('2', 4, 2), ('2', 5, 1), ('2', 4, 0), ('2', 6, 0), ('2', 6, 3), ('3', 2), ('3', 3), ('4', 0), ('2', 7, 3), ('2', 7, 0), ('2', 6, 2), ('4', 1), ('2', 7, 1), ('3', 5), ('3', 4), ('4', 3), ('4', 2), ('3', 6), ('X', 0), ('3', 7), ('4', 5), ('4', 4), ('X', 1), ('4', 6), ('4', 7), ('X', 2), ('X', 3), ('F', 0), ('F', 1), ('O', 0), ('F', 2), ('O', 1), ('F', 3), ('O', 2), ('O', 3))
 BARRIER_AT = 1
 BPAD = 40
 
@@ -43,10 +43,11 @@
         real = np.concatenate([c, s], axis=2).reshape(parts, -1)
         imag = np.concatenate([-s, c], axis=2).reshape(parts, -1)
         blocks.append(np.concatenate([real, imag], axis=0))
-    table = np.stack(blocks).astype(np.float32)
+    table = np.stack(blocks).astype(np.float32).reshape(groups, 2 * parts, groups, 2, 2, parts // 2)
+    table = table.transpose(0, 4, 3, 1, 2, 5).reshape(groups, 4, 2 * parts, groups * (parts // 2))
     high = table.astype(jnp.bfloat16)
     low = (table - high.astype(np.float32)).astype(jnp.bfloat16)
-    return jnp.asarray(np.concatenate([high, low, high], axis=2))
+    return jnp.asarray(np.concatenate([high, low, high], axis=3))
 
 
 def flip(i, pairing):
@@ -55,12 +56,12 @@
 
 def kernel(
     parts, angles, spokes, side,
-    count_ref, angle_ref, block_ref,
+    count_ref, angle_ref, block_ref, ztab_ref,
     kdata_hbm, interp_hbm, sens_hbm, plane_hbm,
-    out_hbm,
+    out_ref,
     kd, itp, sens_v, plane, tab, sensp, senso, binned, spread, other, half,
-    img, r2x, r2y, r3, r4, xbuf, rx, gath,
-    load_sem, sens_send, sens_recv, send_sem, seg_recv, recv_sem, own_send, own_recv, kz_send, kz_recv, out_sem,
+    img, r2x, r2y, r3, r4, xbuf, rx, gath, total, kzout,
+    load_sem, sens_send, sens_recv, send_sem, seg_recv, recv_sem, own_send, own_recv, kz_send, kz_recv,
 ):
     segs = 4
     seg = 128
@@ -351,9 +352,11 @@
             device_id=sibling, device_id_type=MESH,
         )
 
+    def gath_rows(slot, kr):
+        return pl.ds(pl.multiple_of((slot * 4 + kr) * 128, 128), 128)
+
     def kz_remote(n, kr):
-        slot = far if n else group
-        where = gath.at[slot, kr % 2, :, pl.ds(kr // 2 * 8, 8)]
+        where = gath.at[gath_rows(far if n else group, kr)]
         return pltpu.make_async_remote_copy(
             src_ref=where, dst_ref=where,
             send_sem=kz_send.at[n], recv_sem=kz_recv.at[n, kr],
@@ -361,28 +364,46 @@
         )
 
     def finish(kr):
-        k, r = kr // 2, kr % 2
         for n in range(1, 8):
             arrived(n, kr).wait_recv()
         for s in range(4):
             for h in range(2):
-                gath[group, r, h, part_of(s, k, True)] = xbuf[0, kr, 0, s, h] + rx[2, kr, s, h]
-                gath[group, r, h, part_of(s, k, False)] = rx[4, kr, s, h] + rx[6, kr, s, h]
-                gath[far, r, h, part_of(s, k, True)] = rx[1, kr, s, h] + rx[3, kr, s, h]
-                gath[far, r, h, part_of(s, k, False)] = rx[5, kr, s, h] + rx[7, kr, s, h]
+                for slot, mine, value in (
+                    (group, True, xbuf[0, kr, 0, s, h] + rx[2, kr, s, h]),
+                    (group, False, rx[4, kr, s, h] + rx[6, kr, s, h]),
+                    (far, True, rx[1, kr, s, h] + rx[3, kr, s, h]),
+                    (far, False, rx[5, kr, s, h] + rx[7, kr, s, h]),
+                ):
+                    start = (slot * 4 + kr) * 128 + h * 64 + part_of(s, 0, mine)
+                    gath[pl.ds(start, 8, stride=8), :] = value
         for n in range(2):
             kz_remote(n, kr).start()
 
-    def out_copy(kr):
-        rows = (slice(None), kr % 2, slice(None), pl.ds(kr // 2 * 8, 8))
-        return pltpu.make_async_copy(gath.at[rows], out_hbm.at[rows], out_sem.at[kr])
-
-    def put(kr):
+    def put(kr, first, last_one):
         for n in range(2):
             kz_remote(n, kr).wait_recv()
-        out_copy(kr).start()
-
-    for what, *where in PLAN:
+        for h in range(2):
+            rows = []
+            for g in range(4):
+                base = (g * 4 + kr) * 128 + h * 64
+                rows.append(jnp.concatenate([gath[base + yy * 8 : base + yy * 8 + 8, :] for yy in range(8)], axis=1))
+            stacked = jnp.concatenate(rows, axis=0)
+            high = stacked.astype(BF16)
+            low = (stacked - high.astype(F32)).astype(BF16)
+            got = jnp.dot(
+                ztab_ref[group, kr], jnp.concatenate([high, high, low], axis=0), preferred_element_type=F32
+            )
+            if not first:
+                got = got + total[h]
+            if not last_one:
+                total[h] = got
+                continue
+            for yy in range(8):
+                kzout[h, pl.ds(yy, 2 * parts, stride=8), :] = got[:, yy * seg : (yy + 1) * seg]
+            out_ref[:, :, :, h * seg : (h + 1) * seg] = kzout[h].reshape(2, parts, 8, seg)
+
+    begun = [what for what, *where in PLAN].index("O")
+    for n, (what, *where) in enumerate(PLAN):
         if what == "M":
             make(where[1], where[0])
         elif what == "2":
@@ -392,7 +413,7 @@
         elif what == "F":
             finish(*where)
         elif what == "O":
-            put(*where)
+            put(*where, n == begun, n == len(PLAN) - 1)
         else:
             step(int(what), *where)
 
@@ -412,23 +433,7 @@
     for n in range(1, 8):
         sent_all(rx.at[n], own_send.at[n], own_recv.at[n, 0], sibling)
     for n in range(2):
-        sent_all(gath.at[group], kz_send.at[n], kz_recv.at[n, 0], sibling)
-    for kr in range(4):
-        out_copy(kr).wait()
-
-
-def kz_kernel(parts, ztab_ref, gath, out_ref, kzout):
-    group = lax.axis_index("kz")
-    for yy in range(8):
-        pieces = [gath[g, r, 0, :, yy, :] for g in range(4) for r in range(2)]
-        stacked = jnp.concatenate(pieces, axis=0)
-        high = stacked.astype(BF16)
-        low = (stacked - high.astype(F32)).astype(BF16)
-        got = jnp.dot(
-            ztab_ref[group], jnp.concatenate([high, high, low], axis=0), preferred_element_type=F32
-        )
-        kzout[pl.ds(yy, 2 * parts, stride=8), :] = got
-    out_ref[...] = kzout[...].reshape(2, parts, 8, kzout.shape[1])
+        sent_all(gath.at[pl.ds(0, 512)], kz_send.at[n], kz_recv.at[n, 0], sibling)
 
 
 def per_device(kdata, spoke_angle, spoke_count, block_index, interp, sens_maps):
@@ -439,11 +444,11 @@
     hits = angles * segs
     any_spec = pl.BlockSpec(memory_space=pl.ANY)
     vmem_spec = pl.BlockSpec(memory_space=pltpu.VMEM)
-    gathered = pl.pallas_call(
+    return pl.pallas_call(
         functools.partial(kernel, parts, angles, spokes, side),
-        out_shape=jax.ShapeDtypeStruct((4, 2, 2, parts, 8, seg), F32),
-        in_specs=[pl.BlockSpec(memory_space=pltpu.SMEM)] + [vmem_spec] * 2 + [any_spec] * 4,
-        out_specs=any_spec,
+        out_shape=jax.ShapeDtypeStruct((2, parts, 8, side), F32),
+        in_specs=[pl.BlockSpec(memory_space=pltpu.SMEM)] + [vmem_spec] * 3 + [any_spec] * 4,
+        out_specs=vmem_spec,
         scratch_shapes=[
             pltpu.VMEM((2, parts, spokes, samples), BF16),
             pltpu.VMEM((angles, segs, seg, seg), BF16),
@@ -463,7 +468,9 @@
             pltpu.VMEM((4, 8, 2, 16, seg), F32),
             pltpu.VMEM((2, 4, 2, 4, 2, 8, seg), F32),
             pltpu.VMEM((8, 4, 4, 2, 8, seg), F32),
-            pltpu.VMEM((4, 2, 2, parts, 8, seg), F32),
+            pltpu.VMEM((4 * 4 * 128, seg), F32),
+            pltpu.VMEM((2, 2 * parts, 8 * seg), F32),
+            pltpu.VMEM((2, 2 * parts * 8, seg), F32),
             pltpu.SemaphoreType.DMA((10,)),
             pltpu.SemaphoreType.DMA((2, 4)),
             pltpu.SemaphoreType.DMA((2, 4)),
@@ -474,7 +481,6 @@
             pltpu.SemaphoreType.DMA((8, 4)),
             pltpu.SemaphoreType.DMA((2,)),
             pltpu.SemaphoreType.DMA((2, 4)),
-            pltpu.SemaphoreType.DMA((4,)),
         ],
         compiler_params=pltpu.CompilerParams(
             collective_id=0, has_side_effects=True, vmem_limit_bytes=56 << 20
@@ -483,23 +489,12 @@
         spoke_count,
         spoke_angle.reshape(1, spokes),
         block_index.T,
+        kz_table(4, parts),
         kdata[:, :, 0],
         interp,
         sens_maps[:, 0],
         plane_table(side),
     )
-    return pl.pallas_call(
-        functools.partial(kz_kernel, parts),
-        grid=(2,),
-        out_shape=jax.ShapeDtypeStruct((2, parts, 8, side), F32),
-        in_specs=[
-            pl.BlockSpec((4, 2 * parts, 24 * parts), lambda h: (0, 0, 0)),
-            pl.BlockSpec((4, 2, 1, parts, 8, seg), lambda h: (0, 0, h, 0, 0, 0)),
-        ],
-        out_specs=pl.BlockSpec((2, parts, 8, seg), lambda h: (0, 0, 0, h)),
-        scratch_shapes=[pltpu.VMEM((2 * parts * 8, seg), F32)],
-    )(kz_table(4, parts), gathered)
-
 
 def solution(mesh):
     placed = (

time: 62.8 us -> 62.4 us (level)
  Pallas kernels: 62.6 us -> 60.6 us
  local copies, waits for them, and re-layouts: 0 us -> 1.67 us
    pallas_call x1 -> x0, Pallas kernels: 2.62 us -> none  [per_device(): pl.pallas_call(functools.partial(kz_kernel, parts), grid=(2,), out_shape=...]
    unnamed x0 -> x1, local copies, waits for them, and re-layouts: none -> 1.67 us
    pallas_call x1, Pallas kernels: 60 us -> 60.6 us  [per_device(): pl.pallas_call(functools.partial(kernel, parts, angles, spokes, side), ou...]
where the time goes in v7:
time: 62.4 us; the launch traced here: 62.3 us
  Pallas kernels  60.6 us (97%)
  local copies, waits for them, and re-layouts  1.67 us (3%)
    pallas_call x1, Pallas kernels, per_device(): pl.pallas_call(functools.partial(kernel, parts, angles, spokes, side), ou...  60.6 us
    unnamed x1, local copies, waits for them, and re-layouts  1.67 us

profile of v7, /device:TPU:1, one launch (start us, length us, event | category | flops | bytes accessed | tf_op | source)
XLA Modules:
  0.0 62.3 jit_solution(6790150601389939822)
XLA Ops:
  0.0 60.6 %shard_map.82 = f32[2,16,8,256]{3,2,1,0:T(8,128)} custom-call(s32[16]{0:T(128)} %count_ref.1, s32[1,256]{1,0:T(1,128)} %bitcast.7, s32[4,64]{1,0:T(4,128)} %bitcast.6, bf16[4,4,32,96]{3,2,1,0:T(8,128)(2,1)} %constant.4.clone.ztab_ref, bf16[2,16,256,512]{3,2,1,0:T(8,128)(2,1)} %bitcast.4, bf16[64,4,128,128]{3,2,1,0:T(8,128)(2,1)} %interp_hbm.1, ...), custom_call_target="tpu_custom_call" | custom-call | tf_op jit(solution)/shard_map/pallas_call | solution.py:447
  60.6 1.7 %copy.10 = f32[2,16,8,256]{3,2,1,0:T(8,128)} copy(f32[2,16,8,256]{3,2,1,0:T(8,128)} %shard_map.82) | data formatting | bytes 524288

commit v8 on v7

--- a/solution.py
+++ b/solution.py
@@ -13,7 +13,7 @@
 MESH = pl.DeviceIdType.MESH
 
 PLAN = (('M', 0, 2), ('M', 0, 1), ('M', 0, 3), ('2', 1, 2), ('2', 0, 3), ('2', 0, 1), ('M', 0, 0), ('2', 1, 1), ('2', 3, 0), ('2', 1, 3), ('2', 2, 1), ('2', 0, 2), ('2', 3, 1), ('2', 2, 2), ('2', 2, 3), ('2', 0, 0), ('2', 3, 2), ('2', 1, 0), ('M', 1, 2), ('2', 7, 2), ('M', 1, 3), ('2', 2, 0), ('2', 4, 3), ('M', 1, 1), ('2', 3, 3), ('M', 1, 0), ('2', 5, 0), ('2', 6, 1), ('3', 0), ('2', 5, 2), ('2', 5, 3), ('3', 1), ('2', 4, 1), ('2', 4, 2), ('2', 5, 1), ('2', 4, 0), ('2', 6, 0), ('2', 6, 3), ('3', 2), ('3', 3), ('4', 0), ('2', 7, 3), ('2', 7, 0), ('2', 6, 2), ('4', 1), ('2', 7, 1), ('3', 5), ('3', 4), ('4', 3), ('4', 2), ('3', 6), ('X', 0), ('3', 7), ('4', 5), ('4', 4), ('X', 1), ('4', 6), ('4', 7), ('X', 2), ('X', 3), ('F', 0), ('F', 1), ('O', 0), ('F', 2), ('O', 1), ('F', 3), ('O', 2), ('O', 3))
-BARRIER_AT = 1
+BARRIER_AT = 0
 BPAD = 40
 
 STREAMS = ((True, 1), (True, 3), (False, 1), (False, 3))
@@ -61,7 +61,7 @@
     out_ref,
     kd, itp, sens_v, plane, tab, sensp, senso, binned, spread, other, half,
     img, r2x, r2y, r3, r4, xbuf, rx, gath, total, kzout,
-    load_sem, sens_send, sens_recv, send_sem, seg_recv, recv_sem, own_send, own_recv, kz_send, kz_recv,
+    load_sem, sens_send, sens_recv, send_sem, seg_recv, recv_sem, own_send, own_recv, kz_send, kz_recv, round_sem,
 ):
     segs = 4
     seg = 128
@@ -112,8 +112,7 @@
 
     barrier = pltpu.get_barrier_semaphore()
     turns = [(0, 0), (0, 1), (1, 0), (1, 1)]
-    peers = [dev(*stream, *turn) for stream in STREAMS for turn in turns]
-    peers += [zdev(*turn) for turn in turns[1:]] + [sibling]
+    peers = [dev(*stream) for stream in STREAMS] + [zdev(1, 0), zdev(1, 1), sibling]
     for peer in peers:
         pl.semaphore_signal(barrier, inc=1, device_id=peer, device_id_type=MESH)
 
@@ -173,6 +172,8 @@
     pl.semaphore_wait(barrier, len(peers))
     for s in range(4):
         sens_copy(s).start()
+    for peer in peers:
+        pl.semaphore_signal(round_sem.at[0], inc=1, device_id=peer, device_id_type=MESH)
     lax.fori_loop(BARRIER_AT, 4, bin_some, 0)
 
     def spread_some(q, carry):
@@ -202,11 +203,15 @@
         for s in range(4):
             for r in range(2):
                 seg_copy(s, k, r).start()
+    pl.semaphore_wait(round_sem.at[0], len(peers))
+    for peer in peers:
+        pl.semaphore_signal(round_sem.at[1], inc=1, device_id=peer, device_id_type=MESH)
     for s in range(4):
         sens_copy(s).wait_recv()
         sens_pass(s, core).start()
     for s in range(4):
         sens_pass(s, 1 - core).wait_recv()
+    pl.semaphore_wait(round_sem.at[1], len(peers))
 
     def slots(pairing):
         return (1, 0, 1, 3) if pairing == 1 else (2, 1, 0, 1)
@@ -481,6 +486,7 @@
             pltpu.SemaphoreType.DMA((8, 4)),
             pltpu.SemaphoreType.DMA((2,)),
             pltpu.SemaphoreType.DMA((2, 4)),
+            pltpu.SemaphoreType.REGULAR((2,)),
         ],
         compiler_params=pltpu.CompilerParams(
             collective_id=0, has_side_effects=True, vmem_limit_bytes=56 << 20

time: 62.4 us -> 61.9 us (level)
  no operation moved by 1% of the time
where the time goes in v8:
time: 61.9 us; the launch traced here: 61.8 us
  Pallas kernels  60.1 us (97%)
  local copies, waits for them, and re-layouts  1.67 us (3%)
    pallas_call x1, Pallas kernels, per_device(): pl.pallas_call(functools.partial(kernel, parts, angles, spokes, side), ou...  60.1 us
    unnamed x1, local copies, waits for them, and re-layouts  1.67 us

profile of v8, /device:TPU:1, one launch (start us, length us, event | category | flops | bytes accessed | tf_op | source)
XLA Modules:
  0.0 61.8 jit_solution(13186352970403172820)
XLA Ops:
  0.0 60.1 %shard_map.82 = f32[2,16,8,256]{3,2,1,0:T(8,128)} custom-call(s32[16]{0:T(128)} %count_ref.1, s32[1,256]{1,0:T(1,128)} %bitcast.7, s32[4,64]{1,0:T(4,128)} %bitcast.6, bf16[4,4,32,96]{3,2,1,0:T(8,128)(2,1)} %constant.4.clone.ztab_ref, bf16[2,16,256,512]{3,2,1,0:T(8,128)(2,1)} %bitcast.4, bf16[64,4,128,128]{3,2,1,0:T(8,128)(2,1)} %interp_hbm.1, ...), custom_call_target="tpu_custom_call" | custom-call | tf_op jit(solution)/shard_map/pallas_call | solution.py:452
  60.1 1.7 %copy.10 = f32[2,16,8,256]{3,2,1,0:T(8,128)} copy(f32[2,16,8,256]{3,2,1,0:T(8,128)} %shard_map.82) | data formatting | bytes 524288

commit v9 on v8

--- a/solution.py
+++ b/solution.py
@@ -12,7 +12,7 @@
 BF16 = jnp.bfloat16
 MESH = pl.DeviceIdType.MESH
 
-PLAN = (('M', 0, 2), ('M', 0, 1), ('M', 0, 3), ('2', 1, 2), ('2', 0, 3), ('2', 0, 1), ('M', 0, 0), ('2', 1, 1), ('2', 3, 0), ('2', 1, 3), ('2', 2, 1), ('2', 0, 2), ('2', 3, 1), ('2', 2, 2), ('2', 2, 3), ('2', 0, 0), ('2', 3, 2), ('2', 1, 0), ('M', 1, 2), ('2', 7, 2), ('M', 1, 3), ('2', 2, 0), ('2', 4, 3), ('M', 1, 1), ('2', 3, 3), ('M', 1, 0), ('2', 5, 0), ('2', 6, 1), ('3', 0), ('2', 5, 2), ('2', 5, 3), ('3', 1), ('2', 4, 1), ('2', 4, 2), ('2', 5, 1), ('2', 4, 0), ('2', 6, 0), ('2', 6, 3), ('3', 2), ('3', 3), ('4', 0), ('2', 7, 3), ('2', 7, 0), ('2', 6, 2), ('4', 1), ('2', 7, 1), ('3', 5), ('3', 4), ('4', 3), ('4', 2), ('3', 6), ('X', 0), ('3', 7), ('4', 5), ('4', 4), ('X', 1), ('4', 6), ('4', 7), ('X', 2), ('X', 3), ('F', 0), ('F', 1), ('O', 0), ('F', 2), ('O', 1), ('F', 3), ('O', 2), ('O', 3))
+PLAN = (('M', 0, 2), ('M', 0, 1), ('2', 1, 1), ('M', 0, 3), ('2', 1, 3), ('2', 0, 3), ('2', 0, 2), ('M', 0, 0), ('2', 0, 0), ('2', 1, 0), ('2', 2, 0), ('2', 1, 2), ('2', 0, 1), ('2', 2, 1), ('2', 3, 2), ('2', 3, 3), ('M', 1, 1), ('2', 3, 1), ('2', 2, 2), ('2', 2, 3), ('2', 3, 0), ('M', 1, 0), ('M', 1, 3), ('2', 4, 0), ('3', 0), ('3', 1), ('2', 7, 1), ('M', 1, 2), ('2', 6, 2), ('2', 4, 2), ('2', 6, 0), ('2', 5, 3), ('2', 4, 3), ('3', 2), ('2', 5, 2), ('2', 4, 1), ('2', 6, 1), ('2', 6, 3), ('2', 5, 1), ('2', 5, 0), ('3', 3), ('4', 0), ('4', 1), ('2', 7, 0), ('3', 4), ('2', 7, 2), ('4', 2), ('2', 7, 3), ('3', 5), ('4', 3), ('3', 6), ('X', 0), ('4', 4), ('3', 7), ('4', 5), ('X', 1), ('4', 6), ('4', 7), ('X', 2), ('F', 0), ('X', 3), ('F', 1), ('O', 0), ('F', 2), ('O', 1), ('F', 3), ('O', 2), ('O', 3))
 BARRIER_AT = 0
 BPAD = 40
 
@@ -405,7 +405,7 @@
                 continue
             for yy in range(8):
                 kzout[h, pl.ds(yy, 2 * parts, stride=8), :] = got[:, yy * seg : (yy + 1) * seg]
-            out_ref[:, :, :, h * seg : (h + 1) * seg] = kzout[h].reshape(2, parts, 8, seg)
+            out_ref[:, :, :, h * seg : (h + 1) * seg] = kzout[h, 0 : 2 * parts * 8].reshape(2, parts, 8, seg)
 
     begun = [what for what, *where in PLAN].index("O")
     for n, (what, *where) in enumerate(PLAN):
@@ -462,8 +462,8 @@
             pltpu.VMEM((2, 2 * side, 2 * hits), BF16),
             pltpu.VMEM((2, side, side), F32),
             pltpu.VMEM((4, 2, side, side), F32),
-            pltpu.VMEM((segs * angles * BPAD, seg), F32),
-            pltpu.VMEM((2 * parts * (hits + 8), seg), F32),
+            pltpu.VMEM(((segs * angles + 1) * BPAD, seg), F32),
+            pltpu.VMEM(((2 * parts + 1) * (hits + 8), seg), F32),
             pltpu.VMEM((4, 2, 2, hits, seg), F32),
             pltpu.VMEM((2, side, 2 * side), BF16),
             pltpu.VMEM((4, 8, 4, 4, 16, seg), F32),
@@ -473,9 +473,9 @@
             pltpu.VMEM((4, 8, 2, 16, seg), F32),
             pltpu.VMEM((2, 4, 2, 4, 2, 8, seg), F32),
             pltpu.VMEM((8, 4, 4, 2, 8, seg), F32),
-            pltpu.VMEM((4 * 4 * 128, seg), F32),
+            pltpu.VMEM((4 * 4 * 128 + 8, seg), F32),
             pltpu.VMEM((2, 2 * parts, 8 * seg), F32),
-            pltpu.VMEM((2, 2 * parts * 8, seg), F32),
+            pltpu.VMEM((2, 2 * parts * 8 + 8, seg), F32),
             pltpu.SemaphoreType.DMA((10,)),
             pltpu.SemaphoreType.DMA((2, 4)),
             pltpu.SemaphoreType.DMA((2, 4)),

time: 61.9 us -> 61.4 us (level)
  no operation moved by 1% of the time
where the time goes in v9:
time: 61.4 us; the launch traced here: 61.3 us
  Pallas kernels  59.6 us (97%)
  local copies, waits for them, and re-layouts  1.67 us (3%)
    pallas_call x1, Pallas kernels, per_device(): pl.pallas_call(functools.partial(kernel, parts, angles, spokes, side), ou...  59.6 us
    unnamed x1, local copies, waits for them, and re-layouts  1.67 us

profile of v9, /device:TPU:1, one launch (start us, length us, event | category | flops | bytes accessed | tf_op | source)
XLA Modules:
  0.0 61.3 jit_solution(1561940876371389784)
XLA Ops:
  0.0 59.6 %shard_map.82 = f32[2,16,8,256]{3,2,1,0:T(8,128)} custom-call(s32[16]{0:T(128)} %count_ref.1, s32[1,256]{1,0:T(1,128)} %bitcast.7, s32[4,64]{1,0:T(4,128)} %bitcast.6, bf16[4,4,32,96]{3,2,1,0:T(8,128)(2,1)} %constant.4.clone.ztab_ref, bf16[2,16,256,512]{3,2,1,0:T(8,128)(2,1)} %bitcast.4, bf16[64,4,128,128]{3,2,1,0:T(8,128)(2,1)} %interp_hbm.1, ...), custom_call_target="tpu_custom_call" | custom-call | tf_op jit(solution)/shard_map/pallas_call | solution.py:452
  59.6 1.7 %copy.10 = f32[2,16,8,256]{3,2,1,0:T(8,128)} copy(f32[2,16,8,256]{3,2,1,0:T(8,128)} %shard_map.82) | data formatting | bytes 524288

commit v10 on v9

--- a/solution.py
+++ b/solution.py
@@ -107,7 +107,7 @@
         rows = pl.ds(q * (angles // 4), angles // 4)
         return pltpu.make_async_copy(interp_hbm.at[rows], itp.at[rows], load_sem.at[6 + q])
 
-    for copy in loads + [kload(q) for q in range(4)] + [iload(q) for q in range(4)]:
+    for copy in loads[::-1] + [kload(q) for q in range(4)] + [iload(q) for q in range(4)]:
         copy.start()
 
     barrier = pltpu.get_barrier_semaphore()
@@ -116,8 +116,7 @@
     for peer in peers:
         pl.semaphore_signal(barrier, inc=1, device_id=peer, device_id_type=MESH)
 
-    for copy in loads:
-        copy.wait()
+    loads[1].wait()
     row = lax.broadcasted_iota(jnp.int32, (side, side), 0)
     col = lax.broadcasted_iota(jnp.int32, (side, side), 1)
     perm = jnp.where(jnp.bitwise_xor(row, col) == coil * 8, 1.0, 0.0).astype(BF16)
@@ -138,6 +137,7 @@
             device_id=sibling, device_id_type=MESH,
         )
 
+    loads[0].wait()
     cos_p = jnp.dot(perm, plane[0:side, 0:side], preferred_element_type=F32).astype(BF16)
     sin_p = jnp.dot(perm, plane[side : 2 * side, 0:side], preferred_element_type=F32).astype(BF16)
     blocks = jnp.concatenate([block_ref[g : g + 1, :] for g in range(segs)], axis=1)

time: 61.4 us -> 61.4 us (level)
  no operation moved by 1% of the time
where the time goes in v10:
time: 61.4 us; the launch traced here: 61.3 us
  Pallas kernels  59.6 us (97%)
  local copies, waits for them, and re-layouts  1.67 us (3%)
    pallas_call x1, Pallas kernels, per_device(): pl.pallas_call(functools.partial(kernel, parts, angles, spokes, side), ou...  59.6 us
    unnamed x1, local copies, waits for them, and re-layouts  1.67 us

profile of v10, /device:TPU:1, one launch (start us, length us, event | category | flops | bytes accessed | tf_op | source)
XLA Modules:
  0.0 61.3 jit_solution(15309722296077442723)
XLA Ops:
  0.0 59.6 %shard_map.82 = f32[2,16,8,256]{3,2,1,0:T(8,128)} custom-call(s32[16]{0:T(128)} %count_ref.1, s32[1,256]{1,0:T(1,128)} %bitcast.7, s32[4,64]{1,0:T(4,128)} %bitcast.6, bf16[4,4,32,96]{3,2,1,0:T(8,128)(2,1)} %constant.4.clone.ztab_ref, bf16[2,16,256,512]{3,2,1,0:T(8,128)(2,1)} %bitcast.4, bf16[64,4,128,128]{3,2,1,0:T(8,128)(2,1)} %interp_hbm.1, ...), custom_call_target="tpu_custom_call" | custom-call | tf_op jit(solution)/shard_map/pallas_call | solution.py:452
  59.6 1.7 %copy.10 = f32[2,16,8,256]{3,2,1,0:T(8,128)} copy(f32[2,16,8,256]{3,2,1,0:T(8,128)} %shard_map.82) | data formatting | bytes 524288
